TPU v7x, 32 devices: a whole 2x2x4 slice. The times are simulated.
32 devices in a mesh: ctx: 8 (over y, x, core), fsdp: 4 (over z).
Axes of the slice: x: 2, y: 2, z: 4, core: 2. Of those that a mesh axis runs over, the one named last changes fastest.
Arguments:
- tokens: bfloat16 [4, 1536, 1536], P('fsdp', 'ctx'), may hold values from -6 to 6
- positions: int32 [4, 1536], P('fsdp', 'ctx'), may hold values from 0 to 1535, as said below
- qkv_weight: bfloat16 [1, 1536, 3072], P(None, 'fsdp'), as said below
- out_weight: bfloat16 [1, 1536, 1536], P(None, 'fsdp'), may hold values from -2.5 to 2.5
- gate_up_weight: bfloat16 [1, 1536, 2, 4096], P(None, 'fsdp'), may hold values from -0.15625 to 0.15625
- down_weight: bfloat16 [1, 4096, 1536], P(None, 'fsdp'), may hold values from -0.09375 to 0.09375
- attn_gain: bfloat16 [1, 1536], P(None, 'fsdp'), may hold values from 0.5 to 1.5
- ffn_gain: bfloat16 [1, 1536], P(None, 'fsdp'), may hold values from 0.5 to 1.5
- cotangent: float32 [4, 1536, 1536], P('fsdp', 'ctx'), may hold values from -6 to 6
Outputs:
- activations: bfloat16 [4, 1536, 1536], P('fsdp', 'ctx')
- input_grad: float32 [4, 1536, 1536], P('fsdp', 'ctx')
- qkv_grad: float32 [1, 1536, 3072], P(None, 'fsdp')
- out_grad: float32 [1, 1536, 1536], P(None, 'fsdp')
- gate_up_grad: float32 [1, 1536, 2, 4096], P(None, 'fsdp')
- down_grad: float32 [1, 4096, 1536], P(None, 'fsdp')
- attn_gain_grad: float32 [1, 1536], P(None, 'fsdp')
- ffn_gain_grad: float32 [1, 1536], P(None, 'fsdp')
Inputs may be any that keep to these rules, and one draw needn't show every extreme that they name: Each sequence holds every position of 0 to 1535 once. Its rows form aligned blocks of 192 rows; a block holds span c (the 96 positions from c * 96 on, in order) and then span 2 * 8 - 1 - c likewise; c differs between the blocks of a sequence. `qkv_weight`: projection weights of mean zero.
All inputs are finite; a program needn't handle non-finite values.
Results may differ from a plain program's by a relative error of at most 0.017.
The roundings to bfloat16 on the way count: a program that leaves them out, or rounds other values in their place, can miss the bound.
Values may be sent and summed in bfloat16 or wider, within the bound.
A program may use at most 320 MiB of HBM per device.

v0:
```python
import jax
import jax.numpy as jnp
import numpy as np
from jax import lax
from jax.experimental import pallas as pl
from jax.experimental.pallas import tpu as pltpu
from jax.sharding import PartitionSpec as P

HEADS = 16
KV_HEADS = 8
HEAD_DIM = 96
LAYERS = 1


epsilon = 1e-05
rope_base = 100000.0


def angles(place):
    halfway = HEAD_DIM // 2
    frequency = rope_base ** (-(jnp.arange(halfway, dtype=jnp.float32) * 2.0 / HEAD_DIM))
    phases = place.astype(jnp.float32)[:, None] * frequency[None, :]
    phases = jnp.concatenate([phases, phases], axis=-1)
    return (jnp.cos(phases)[:, None, :], jnp.sin(phases)[:, None, :])


def rotate(vectors, cosine, sine):
    halfway = vectors.shape[-1] // 2
    turned = jnp.concatenate([-vectors[..., halfway:], vectors[..., :halfway]], axis=-1)
    return vectors * cosine + turned * sine


def rotate_back(grads, cosine, sine):
    halfway = grads.shape[-1] // 2
    scaled = grads * sine
    return grads * cosine + jnp.concatenate(
        [scaled[..., halfway:], -scaled[..., :halfway]], axis=-1
    )


def normalize(rows, gain):
    factor = lax.rsqrt(jnp.mean(rows * rows, axis=-1, keepdims=True) + epsilon)
    return (rows * factor * gain, factor)


def normalize_back(upstream, rows, factor, gain):
    unit_rows = rows * factor
    gain_grad = jnp.sum(upstream * unit_rows, axis=0)
    scaled = upstream * gain
    row_inner = jnp.mean(scaled * unit_rows, axis=-1, keepdims=True)
    return (factor * (scaled - unit_rows * row_inner), gain_grad)


def split_blocks(queries, keys_all, values_all, key_place):
    rows = queries.shape[0]
    half = rows // 2
    shards = key_place.shape[0] // rows
    key_blocks = keys_all.reshape(shards, 2, half, KV_HEADS, HEAD_DIM)
    value_blocks = values_all.reshape(shards, 2, half, KV_HEADS, HEAD_DIM)
    place_blocks = key_place.reshape(shards, 2, half)
    return (key_blocks, value_blocks, place_blocks)


def scores_of(queries, key_block, place_block, query_place):
    scaling = HEAD_DIM ** (-0.5)
    scores = (
        jnp.einsum("rkgd,skd->kgrs", queries, key_block, preferred_element_type=jnp.float32)
        * scaling
    )
    allowed = place_block[None, None, None, :] <= query_place[None, None, :, None]
    return (scores, allowed)


def reachable(place_block, query_place):
    return jnp.min(place_block) <= jnp.max(query_place)


def attention_forward(queries, keys_all, values_all, query_place, key_place):
    key_blocks, value_blocks, place_blocks = split_blocks(queries, keys_all, values_all, key_place)
    rows = queries.shape[0]
    half = rows // 2
    groups = HEADS // KV_HEADS
    query_spans = queries.reshape(2, half, KV_HEADS, groups, HEAD_DIM)
    place_spans = query_place.reshape(2, half)

    def sweep_max(carry, inputs):
        key_block, place_block = inputs
        updated_all = []
        for span in range(2):
            state = carry[span]
            for part in range(2):

                def live(current, span=span, part=part):
                    maximum, total = current
                    scores, allowed = scores_of(
                        query_spans[span], key_block[part], place_block[part], place_spans[span]
                    )
                    masked = jnp.where(allowed, scores, -1e30)
                    updated = jnp.maximum(maximum, jnp.max(masked, axis=-1))
                    weights_now = jnp.where(allowed, jnp.exp(masked - updated[..., None]), 0.0)
                    return (
                        updated,
                        total * jnp.exp(maximum - updated) + jnp.sum(weights_now, axis=-1),
                    )

                state = lax.cond(
                    reachable(place_block[part], place_spans[span]),
                    live,
                    lambda current: current,
                    state,
                )
            updated_all.append(state)
        return (tuple(updated_all), None)

    start_max = jnp.full((KV_HEADS, groups, half), -1e30, jnp.float32)
    start_total = jnp.zeros((KV_HEADS, groups, half), jnp.float32)
    start = ((start_max, start_total), (start_max, start_total))
    finals, unused = lax.scan(sweep_max, start, (key_blocks, place_blocks))
    logsum_spans = [finals[span][0] + jnp.log(finals[span][1]) for span in range(2)]

    def sweep_out(results, inputs):
        key_block, value_block, place_block = inputs
        updated_all = []
        for span in range(2):
            result = results[span]
            for part in range(2):

                def live(current, span=span, part=part):
                    scores, allowed = scores_of(
                        query_spans[span], key_block[part], place_block[part], place_spans[span]
                    )
                    softmax_rows = jnp.where(
                        allowed, jnp.exp(scores - logsum_spans[span][..., None]), 0.0
                    ).astype(jnp.bfloat16)
                    return current + jnp.einsum(
                        "kgrs,skd->rkgd",
                        softmax_rows,
                        value_block[part],
                        preferred_element_type=jnp.float32,
                    )

                result = lax.cond(
                    reachable(place_block[part], place_spans[span]),
                    live,
                    lambda current: current,
                    result,
                )
            updated_all.append(result)
        return (tuple(updated_all), None)

    start_out = jnp.zeros((half, KV_HEADS, groups, HEAD_DIM), jnp.float32)
    outs, unused_out = lax.scan(
        sweep_out, (start_out, start_out), (key_blocks, value_blocks, place_blocks)
    )
    logsum = jnp.concatenate(logsum_spans, axis=-1)
    attended = jnp.concatenate([outs[0], outs[1]], axis=0)
    return (logsum, attended)


def attention_backward(
    queries, keys_all, values_all, query_place, key_place, logsum, attended_grad, row_inner
):
    key_blocks, value_blocks, place_blocks = split_blocks(queries, keys_all, values_all, key_place)
    rows = queries.shape[0]
    half = rows // 2
    groups = HEADS // KV_HEADS
    scaling = HEAD_DIM ** (-0.5)
    query_spans = queries.reshape(2, half, KV_HEADS, groups, HEAD_DIM)
    place_spans = query_place.reshape(2, half)
    grad_spans = attended_grad.reshape(2, half, KV_HEADS, groups, HEAD_DIM)
    logsum_spans = logsum.reshape(KV_HEADS, groups, 2, half)
    inner_spans = row_inner.reshape(KV_HEADS, groups, 2, half)

    def sweep_back(query_grads, inputs):
        key_block, value_block, place_block = inputs
        query_grads = list(query_grads)
        key_parts = []
        value_parts = []
        for part in range(2):
            key_acc = jnp.zeros((half, KV_HEADS, HEAD_DIM), jnp.float32)
            value_acc = jnp.zeros((half, KV_HEADS, HEAD_DIM), jnp.float32)
            for span in range(2):

                def live(current, span=span, part=part):
                    query_grad, key_grad, value_grad = current
                    scores, allowed = scores_of(
                        query_spans[span], key_block[part], place_block[part], place_spans[span]
                    )
                    softmax_rows = jnp.where(
                        allowed, jnp.exp(scores - logsum_spans[:, :, span][..., None]), 0.0
                    )
                    rounded = softmax_rows.astype(jnp.bfloat16)
                    weight_grad = jnp.einsum(
                        "rkgd,skd->kgrs",
                        grad_spans[span],
                        value_block[part],
                        preferred_element_type=jnp.float32,
                    )
                    score_grad = (
                        softmax_rows * (weight_grad - inner_spans[:, :, span][..., None])
                    ).astype(jnp.bfloat16)
                    query_grad = (
                        query_grad
                        + jnp.einsum(
                            "kgrs,skd->rkgd",
                            score_grad,
                            key_block[part],
                            preferred_element_type=jnp.float32,
                        )
                        * scaling
                    )
                    key_grad = (
                        key_grad
                        + jnp.einsum(
                            "kgrs,rkgd->skd",
                            score_grad,
                            query_spans[span],
                            preferred_element_type=jnp.float32,
                        )
                        * scaling
                    )
                    value_grad = value_grad + jnp.einsum(
                        "kgrs,rkgd->skd",
                        rounded,
                        grad_spans[span],
                        preferred_element_type=jnp.float32,
                    )
                    return (query_grad, key_grad, value_grad)

                state = (query_grads[span], key_acc, value_acc)
                state = lax.cond(
                    reachable(place_block[part], place_spans[span]),
                    live,
                    lambda current: current,
                    state,
                )
                query_grads[span], key_acc, value_acc = state
            key_parts.append(key_acc)
            value_parts.append(value_acc)
        key_out = jnp.concatenate(key_parts, axis=0)
        value_out = jnp.concatenate(value_parts, axis=0)
        return (tuple(query_grads), (key_out, value_out))

    start_grad = jnp.zeros((half, KV_HEADS, groups, HEAD_DIM), jnp.float32)
    query_pair, (key_grads, value_grads) = lax.scan(
        sweep_back, (start_grad, start_grad), (key_blocks, value_blocks, place_blocks)
    )
    query_grad = jnp.concatenate([query_pair[0], query_pair[1]], axis=0)
    return (
        query_grad,
        key_grads.reshape(-1, KV_HEADS, HEAD_DIM),
        value_grads.reshape(-1, KV_HEADS, HEAD_DIM),
    )


def fetch_layer(qkv_weight, out_weight, gate_up_weight, down_weight, attn_gain, ffn_gain, layer_id):
    return (
        lax.all_gather(qkv_weight[layer_id], "fsdp", axis=0, tiled=True),
        lax.all_gather(out_weight[layer_id], "fsdp", axis=0, tiled=True),
        lax.all_gather(gate_up_weight[layer_id], "fsdp", axis=0, tiled=True),
        lax.all_gather(down_weight[layer_id], "fsdp", axis=0, tiled=True),
        lax.all_gather(attn_gain[layer_id], "fsdp", axis=0, tiled=True),
        lax.all_gather(ffn_gain[layer_id], "fsdp", axis=0, tiled=True),
    )


def fetch_again(qkv_weight, out_weight, gate_up_weight, down_weight, attn_gain, ffn_gain, layer_id):
    return (
        lax.all_gather(qkv_weight[layer_id], "fsdp", axis=0, tiled=True),
        lax.all_gather(out_weight[layer_id], "fsdp", axis=0, tiled=True),
        lax.all_gather(gate_up_weight[layer_id], "fsdp", axis=0, tiled=True),
        lax.all_gather(down_weight[layer_id], "fsdp", axis=0, tiled=True),
        lax.all_gather(attn_gain[layer_id], "fsdp", axis=0, tiled=True),
        lax.all_gather(ffn_gain[layer_id], "fsdp", axis=0, tiled=True),
    )


def forward_layer(stream, query_place, key_place, gathered):
    qkv_full, out_full, gate_up_full, down_full, attn_full, ffn_full = gathered
    rows = stream.shape[0]
    groups = HEADS // KV_HEADS
    query_width = HEADS * HEAD_DIM
    key_width = KV_HEADS * HEAD_DIM
    cosine, sine = angles(query_place)
    normed, first_factor = normalize(stream, attn_full.astype(jnp.float32))
    normed = normed.astype(jnp.bfloat16)
    projected = jnp.dot(normed, qkv_full, preferred_element_type=jnp.float32)
    queries = rotate(projected[:, :query_width].reshape(rows, HEADS, HEAD_DIM), cosine, sine)
    queries = queries.reshape(rows, KV_HEADS, groups, HEAD_DIM).astype(jnp.bfloat16)
    keys_local = rotate(
        projected[:, query_width : query_width + key_width].reshape(rows, KV_HEADS, HEAD_DIM),
        cosine,
        sine,
    ).astype(jnp.bfloat16)
    values_local = (
        projected[:, query_width + key_width :]
        .reshape(rows, KV_HEADS, HEAD_DIM)
        .astype(jnp.bfloat16)
    )
    keys_all, values_all = (
        lax.all_gather(keys_local, "ctx", axis=0, tiled=True),
        lax.all_gather(values_local, "ctx", axis=0, tiled=True),
    )
    logsum, attended = attention_forward(queries, keys_all, values_all, query_place, key_place)
    attended_low = attended.reshape(rows, query_width).astype(jnp.bfloat16)
    middle = stream + jnp.dot(attended_low, out_full, preferred_element_type=jnp.float32)
    second, second_factor = normalize(middle, ffn_full.astype(jnp.float32))
    second = second.astype(jnp.bfloat16)
    gate_up = jnp.einsum("rd,dcf->rcf", second, gate_up_full, preferred_element_type=jnp.float32)
    hidden = (jax.nn.silu(gate_up[:, 0]) * gate_up[:, 1]).astype(jnp.bfloat16)
    result = middle + jnp.dot(hidden, down_full, preferred_element_type=jnp.float32)
    stored = (
        stream,
        first_factor,
        normed,
        queries,
        keys_local,
        values_local,
        keys_all,
        values_all,
        logsum,
        attended,
        attended_low,
        middle,
        second_factor,
        second,
        gate_up,
        hidden,
    )
    return (result, stored)


def backward_layer(upstream, stored, gathered, query_place, key_place, keys_all, values_all):
    (
        stream,
        first_factor,
        normed,
        queries,
        keys_local,
        values_local,
        kept_keys,
        kept_values,
        logsum,
        attended,
        attended_low,
        middle,
        second_factor,
        second,
        gate_up,
        hidden,
    ) = stored
    qkv_full, out_full, gate_up_full, down_full, attn_full, ffn_full = gathered
    rows = stream.shape[0]
    groups = HEADS // KV_HEADS
    cosine, sine = angles(query_place)
    upstream_low = upstream.astype(jnp.bfloat16)
    hidden_grad = jnp.einsum(
        "rd,fd->rf", upstream_low, down_full, preferred_element_type=jnp.float32
    )
    gate_part = gate_up[:, 0]
    up_part = gate_up[:, 1]
    sigmoid = jax.nn.sigmoid(gate_part)
    gate_grad = hidden_grad * up_part * sigmoid * (1.0 + gate_part * (1.0 - sigmoid))
    up_grad = hidden_grad * gate_part * sigmoid
    gate_up_low = jnp.stack([gate_grad, up_grad], axis=1).astype(jnp.bfloat16)
    second_grad = jnp.einsum(
        "rcf,dcf->rd", gate_up_low, gate_up_full, preferred_element_type=jnp.float32
    )
    middle_grad, ffn_gain_grad = normalize_back(
        second_grad, middle, second_factor, ffn_full.astype(jnp.float32)
    )
    middle_grad = middle_grad + upstream
    middle_low = middle_grad.astype(jnp.bfloat16)
    attended_grad = jnp.einsum(
        "rd,od->ro", middle_low, out_full, preferred_element_type=jnp.float32
    )
    attended_grad = attended_grad.astype(jnp.bfloat16).reshape(rows, KV_HEADS, groups, HEAD_DIM)
    row_inner = jnp.einsum("rkgd,rkgd->kgr", attended_grad.astype(jnp.float32), attended)
    query_grad, key_grads, value_grads = attention_backward(
        queries, keys_all, values_all, query_place, key_place, logsum, attended_grad, row_inner
    )
    key_grad, value_grad = (
        lax.psum_scatter(key_grads, "ctx", scatter_dimension=0, tiled=True),
        lax.psum_scatter(value_grads, "ctx", scatter_dimension=0, tiled=True),
    )
    query_grad = rotate_back(query_grad.reshape(rows, HEADS, HEAD_DIM), cosine, sine)
    key_grad = rotate_back(key_grad, cosine, sine)
    projected_grad = jnp.concatenate(
        [query_grad.reshape(rows, -1), key_grad.reshape(rows, -1), value_grad.reshape(rows, -1)],
        axis=1,
    ).astype(jnp.bfloat16)
    normed_grad = jnp.einsum(
        "re,de->rd", projected_grad, qkv_full, preferred_element_type=jnp.float32
    )
    stream_grad, attn_gain_grad = normalize_back(
        normed_grad, stream, first_factor, attn_full.astype(jnp.float32)
    )
    stream_grad = stream_grad + middle_grad
    qkv_grad = jnp.einsum("rd,re->de", normed, projected_grad, preferred_element_type=jnp.float32)
    out_grad = jnp.einsum("ro,rd->od", attended_low, middle_low, preferred_element_type=jnp.float32)
    gate_up_grad = jnp.einsum(
        "rd,rcf->dcf", second, gate_up_low, preferred_element_type=jnp.float32
    )
    down_grad = jnp.einsum("rf,rd->fd", hidden, upstream_low, preferred_element_type=jnp.float32)
    sharded = (
        lax.psum_scatter(qkv_grad, "fsdp", scatter_dimension=0, tiled=True),
        lax.psum_scatter(out_grad, "fsdp", scatter_dimension=0, tiled=True),
        lax.psum_scatter(gate_up_grad, "fsdp", scatter_dimension=0, tiled=True),
        lax.psum_scatter(down_grad, "fsdp", scatter_dimension=0, tiled=True),
        lax.psum_scatter(attn_gain_grad, "fsdp", scatter_dimension=0, tiled=True),
        lax.psum_scatter(ffn_gain_grad, "fsdp", scatter_dimension=0, tiled=True),
    )
    totals = lax.psum(
        (sharded[0], sharded[1], sharded[2], sharded[3], sharded[4], sharded[5]), "ctx"
    )
    return (stream_grad, totals)


def body(
    tokens,
    positions,
    qkv_weight,
    out_weight,
    gate_up_weight,
    down_weight,
    attn_gain,
    ffn_gain,
    cotangent,
):
    query_place = positions[0]
    key_place = lax.all_gather(query_place, "ctx", axis=0, tiled=True)
    stream = tokens[0].astype(jnp.float32)
    gathered_list = []
    layer_id = 0
    gathered = fetch_layer(
        qkv_weight, out_weight, gate_up_weight, down_weight, attn_gain, ffn_gain, layer_id
    )
    stream, stored = forward_layer(stream, query_place, key_place, gathered)
    saved = [stored]
    gathered_list.append(gathered)
    activations = stream.astype(jnp.bfloat16)[None]
    upstream = cotangent[0]
    layer_grads = [None] * LAYERS
    for layer_id in reversed(range(LAYERS)):
        stored = saved[layer_id]
        gathered = fetch_again(
            qkv_weight, out_weight, gate_up_weight, down_weight, attn_gain, ffn_gain, layer_id
        )
        keys_all, values_all = (stored[6], stored[7])
        upstream, totals = backward_layer(
            upstream, stored, gathered, query_place, key_place, keys_all, values_all
        )
        layer_grads[layer_id] = totals
    outputs = [jnp.stack([entry[slot] for entry in layer_grads], axis=0) for slot in range(6)]
    return (
        activations,
        upstream[None],
        outputs[0],
        outputs[1],
        outputs[2],
        outputs[3],
        outputs[4],
        outputs[5],
    )


LANES = 128


def spread(heads):
    half = HEAD_DIM // 2
    pad = ((0, 0), (0, 0), (0, 64 - half))
    return jnp.concatenate([jnp.pad(heads[..., :half], pad), jnp.pad(heads[..., half:], pad)], axis=-1)


def gathered_spread(padded):
    half = HEAD_DIM // 2
    return jnp.concatenate([padded[..., :half], padded[..., 64 : 64 + half]], axis=-1)


def turn_parts(spans, rows):
    half = HEAD_DIM // 2
    frequency = rope_base ** (-(np.arange(half, dtype=np.float64) * 2.0 / HEAD_DIM))

    def waves(place):
        phases = place[:, None] * frequency[None, :]
        pad = ((0, 0), (0, 64 - half))
        return np.pad(np.cos(phases), pad), np.pad(np.sin(phases), pad)

    cosine, sine = waves(np.arange(spans) * float(rows))
    parts = (
        np.concatenate([cosine, cosine], axis=1), np.concatenate([-sine, sine], axis=1),
        np.concatenate(waves(np.arange(rows, dtype=np.float64)), axis=1),
    )
    return tuple(jnp.asarray(part, jnp.float32) for part in parts)


def spread_heads(proj):
    lane = lax.broadcasted_iota(jnp.int32, (proj.shape[0], LANES), 1)
    tiles = [proj[:, at * LANES : (at + 1) * LANES] for at in range(3)]

    def put(*pieces):
        out = jnp.zeros_like(tiles[0])
        for tile, source, target, count in pieces:
            shift = (target - source) % LANES
            moved = pltpu.roll(tiles[tile], shift, 1) if shift else tiles[tile]
            out = jnp.where(jnp.logical_and(lane >= target, lane < target + count), moved, out)
        return out

    return (
        put((0, 0, 0, 48), (0, 48, 64, 48)),
        put((0, 96, 0, 32), (1, 0, 32, 16), (1, 16, 64, 48)),
        put((1, 64, 0, 48), (1, 112, 64, 16), (2, 0, 80, 32)),
        put((2, 32, 0, 96)),
    )


def close_halves(head):
    lane = lax.broadcasted_iota(jnp.int32, head.shape, 1)
    return jnp.where(lane < HEAD_DIM // 2, head, pltpu.roll(head, LANES - 64 + HEAD_DIM // 2, 1))


def wave(rows):
    first = lax.broadcasted_iota(jnp.int32, rows.shape, 1) < 64
    other = pltpu.roll(rows, 64, 1)
    return jnp.where(first, rows, other), jnp.where(first, -other, rows)


def nt(left, right):
    return lax.dot_general(left, right, (((1,), (1,)), ((), ())), preferred_element_type=jnp.float32)


def nn(left, right):
    return lax.dot_general(left, right, (((1,), (0,)), ((), ())), preferred_element_type=jnp.float32)


def tn(left, right):
    return lax.dot_general(left, right, (((0,), (0,)), ((), ())), preferred_element_type=jnp.float32)


def causal(width, place):
    key_at = lax.broadcasted_iota(jnp.int32, (2 * width, 2 * width), 0)
    query_at = lax.broadcasted_iota(jnp.int32, (2 * width, 2 * width), 1)
    query_at = jnp.where(query_at >= width, query_at - width, query_at)
    return key_at <= query_at + place * width


def vm(count):
    return [pl.BlockSpec(memory_space=pltpu.VMEM)] * count


MESH = pl.DeviceIdType.MESH


class Place:
    def __init__(self):
        self.me = lax.axis_index("ctx")
        core, x, y = self.me % 2, (self.me // 2) % 2, self.me // 4
        self.dp, self.dx, self.dy = 1 - 2 * core, 2 - 4 * x, 4 - 8 * y
        self.p, self.x, self.y = self.me + self.dp, self.me + self.dx, self.me + self.dy
        self.d = self.x + self.dy
        self.z = lax.axis_index("fsdp")
        self.planes = lax.axis_size("fsdp")
        self.n = lax.axis_size("ctx")


def greet(place, ctx=True, planes=False):
    barrier = pltpu.get_barrier_semaphore()
    count = 0
    if ctx:
        for step in range(1, place.n):
            pl.semaphore_signal(
                barrier, inc=1, device_id={"ctx": lax.rem(place.me + step, place.n)}, device_id_type=MESH
            )
            count += 1
    if planes:
        for step in range(1, place.planes):
            pl.semaphore_signal(
                barrier, inc=1, device_id={"fsdp": lax.rem(place.z + step, place.planes)}, device_id_type=MESH
            )
            count += 1
    pl.semaphore_wait(barrier, count)


def send(source, target, send_sem, recv_sem, **where):
    return pltpu.make_async_remote_copy(
        src_ref=source, dst_ref=target, send_sem=send_sem, recv_sem=recv_sem,
        device_id=where, device_id_type=MESH,
    )


class Gather:
    sems = 14

    def __init__(self, place, own, out, sem):
        self.place, self.own, self.out, self.sem = place, own, out, sem
        self.half = out.shape[1] // 2
        self.started = []
        self.met = False

    def go(self, source, target, index, rank):
        send(source, target, self.sem.at[0, index], self.sem.at[1, index], ctx=rank).start()
        self.started.append(index)

    def whole_block(self, index):
        return index == 6

    def sent(self):
        p = self.place
        for index in self.started:
            part = self.whole(p.me) if self.whole_block(index) else self.part(p.me, 0)
            send(part, part, self.sem.at[0, index], self.sem.at[1, index], ctx=p.p).wait_send()

    def part(self, rank, half):
        return self.out.at[rank, pl.ds(half * self.half, self.half)]

    def whole(self, rank):
        return self.out.at[rank]

    def start(self):
        p = self.place
        keep = pltpu.make_async_copy(self.own, self.whole(p.me), self.sem.at[0, 13])
        keep.start()
        self.keep = keep
        halves = [self.own.at[pl.ds(h * self.half, self.half)] for h in range(2)]
        self.go(halves[0], self.part(p.me, 0), 0, p.x)
        self.go(halves[1], self.part(p.me, 1), 3, p.y)
        self.go(self.own, self.whole(p.me), 6, p.p)
        self.go(halves[1], self.part(p.me, 1), 1, p.x)
        self.go(halves[0], self.part(p.me, 0), 2, p.y)

    def arrived(self, rank, half, index):
        part = self.part(rank, half)
        pltpu.make_async_copy(part, part, self.sem.at[1, index]).wait()
        return part

    def relay(self):
        p = self.place
        part = self.arrived(p.x, 0, 0)
        self.go(part, part, 4, p.y)
        self.go(part, part, 7, p.p)
        part = self.arrived(p.y, 1, 3)
        self.go(part, part, 5, p.x)
        self.go(part, part, 10, p.p)

    def rest(self):
        p = self.place
        for rank, half, index, onward in ((p.x, 1, 1, 8), (p.y, 0, 2, 9), (p.d, 0, 4, 11), (p.d, 1, 5, 12)):
            part = self.arrived(rank, half, index)
            self.go(part, part, onward, p.p)

    def first_partner(self):
        part = self.whole(self.place.p)
        pltpu.make_async_copy(part, part, self.sem.at[1, 6]).wait()
        self.met = True

    def partner(self):
        p = self.place
        if not self.met:
            self.first_partner()
        for rank, half, index in (
            (p.x, 0, 7), (p.y, 1, 10), (p.x, 1, 8), (p.y, 0, 9), (p.d, 0, 11), (p.d, 1, 12),
        ):
            self.arrived(rank + p.dp, half, index)

    def finish(self, kept=False):
        if not kept:
            self.keep.wait()
        self.sent()


class PlaneGather:
    def __init__(self, place, own, out, sem):
        self.place, self.own, self.out, self.sem = place, own, out, sem

    def hop(self, step, up):
        p = self.place
        sign = 1 if up else -1
        source = p.z - sign * step
        target = p.z + sign
        ok = jnp.logical_and(
            jnp.logical_and(source >= 0, source < p.planes),
            jnp.logical_and(target >= 0, target < p.planes),
        )
        source = jnp.clip(source, 0, p.planes - 1)
        target = jnp.clip(target, 0, p.planes - 1)
        block = self.own if step == 0 else self.out.at[source]
        return ok, send(
            block, self.out.at[source], self.sem.at[0 if up else 1, source], self.sem.at[2, source], fsdp=target
        )

    def start(self):
        p = self.place
        self.keep = pltpu.make_async_copy(self.own, self.out.at[p.z], self.sem.at[2, p.z])
        self.keep.start()
        for up in (True, False):
            ok, copy = self.hop(0, up)
            pl.when(ok)(copy.start)

    def got(self, step, up):
        p = self.place
        source = p.z - step if up else p.z + step
        ok = jnp.logical_and(source >= 0, source < p.planes)
        source = jnp.clip(source, 0, p.planes - 1)
        part = self.out.at[source]
        return ok, pltpu.make_async_copy(part, part, self.sem.at[2, source])

    def step(self, number):
        for up in (True, False):
            ok, copy = self.got(number, up)
            pl.when(ok)(copy.wait)
            if number < self.place.planes - 1:
                ok, copy = self.hop(number, up)
                pl.when(ok)(copy.start)

    def finish(self, kept=False):
        if not kept:
            self.keep.wait()
        for number in range(self.place.planes - 1):
            for up in (True, False):
                ok, copy = self.hop(number, up)
                pl.when(ok)(copy.wait_send)


class Exchange:
    def __init__(self, place, blocks, out, sem):
        self.place, self.blocks, self.out, self.sem = place, blocks, out, sem

    def pick(self, rank):
        return self.blocks.at[rank]

    def copy(self, step):
        p = self.place
        rank = lax.rem(p.me + step, p.n)
        return send(self.pick(rank), self.out.at[p.me], self.sem.at[0, step], self.sem.at[1, step], ctx=rank)

    def start(self):
        p = self.place
        for step in range(1, p.n):
            self.copy(step).start()
        self.keep = pltpu.make_async_copy(self.pick(p.me), self.out.at[p.me], self.sem.at[0, 0])
        self.keep.start()

    def finish(self):
        p = self.place
        self.keep.wait()
        for step in range(1, p.n):
            self.copy(step).wait_send()
        for step in range(1, p.n):
            part = self.out.at[lax.rem(p.me + p.n - step, p.n)]
            pltpu.make_async_copy(part, part, self.sem.at[1, step]).wait()


class Share(Exchange):
    def pick(self, rank):
        return self.blocks


class PlaneShare:
    def __init__(self, place, block, out, sem):
        self.place, self.block, self.out, self.sem = place, block, out, sem

    def copy(self, step):
        p = self.place
        plane = lax.rem(p.z + step, p.planes)
        return send(self.block, self.out.at[p.z], self.sem.at[0, step], self.sem.at[1, step], fsdp=plane)

    def start(self):
        p = self.place
        for step in range(1, p.planes):
            self.copy(step).start()
        self.keep = pltpu.make_async_copy(self.block, self.out.at[p.z], self.sem.at[0, 0])
        self.keep.start()

    def finish(self):
        p = self.place
        self.keep.wait()
        for step in range(1, p.planes):
            self.copy(step).wait_send()
        for step in range(1, p.planes):
            part = self.out.at[lax.rem(p.z + p.planes - step, p.planes)]
            pltpu.make_async_copy(part, part, self.sem.at[1, step]).wait()


def anywhere(count):
    return [pl.BlockSpec(memory_space=pl.ANY)] * count


class Reduce:
    sems = 10

    def __init__(self, place, mine, theirs, first, out, second, sem):
        self.place, self.mine, self.theirs, self.first, self.out, self.second, self.sem = (
            place, mine, theirs, first, out, second, sem
        )
        self.half = out.shape[1]
        self.started = []

    def push(self, slot):
        copy = send(
            self.theirs.at[slot], self.first.at[slot], self.sem.at[0, slot], self.sem.at[1, slot], ctx=self.place.p
        )
        copy.start()
        return copy

    def pushed(self):
        for slot in range(4):
            send(
                self.theirs.at[slot], self.first.at[slot], self.sem.at[0, slot], self.sem.at[1, slot],
                ctx=self.place.p,
            ).wait_send()

    def add(self, slot):
        part = self.first.at[slot]
        pltpu.make_async_copy(part, part, self.sem.at[1, slot]).wait()
        self.mine[slot] = self.mine[slot] + self.first[slot].astype(jnp.float32)

    def go(self, index, value, rank):
        self.out[index] = value.astype(jnp.bfloat16)
        self.turned(index, rank).start()
        self.started.append((index, rank))

    def turned(self, index, rank):
        return send(
            self.out.at[index], self.second.at[index], self.sem.at[0, 4 + index], self.sem.at[1, 4 + index], ctx=rank
        )

    def top(self, slot):
        return self.mine[slot, pl.ds(0, self.half), :]

    def low(self, slot):
        return self.mine[slot, pl.ds(self.half, self.half), :]

    def got(self, index):
        part = self.second.at[index]
        pltpu.make_async_copy(part, part, self.sem.at[1, 4 + index]).wait()
        return self.second[index].astype(jnp.float32)

    def across(self):
        self.add(3)
        self.go(1, self.top(3), self.place.x)
        self.go(3, self.low(3), self.place.y)

    def beside(self):
        self.add(1)
        self.go(0, self.top(1), self.place.x)
        self.add(2)
        self.go(2, self.low(2), self.place.y)

    def turn(self):
        self.go(4, self.top(2) + self.got(1), self.place.y)
        self.go(5, self.low(1) + self.got(3), self.place.x)

    def total(self, use):
        self.add(0)
        use(pl.ds(0, self.half), self.top(0) + self.got(0) + self.got(4))
        use(pl.ds(self.half, self.half), self.low(0) + self.got(2) + self.got(5))

    def finish(self):
        self.pushed()
        for index, rank in self.started:
            self.turned(index, rank).wait_send()


def flip(place, i):
    return place.me + (i % 2) * place.dp + ((i // 2) % 2) * place.dx + (i // 4) * place.dy


class HalfGather(Gather):
    sems = 16

    def __init__(self, place, own, out, sem):
        self.place, self.own, self.out, self.sem = place, own, out, sem
        self.half = out.shape[1]
        self.started = []
        self.met = False

    def part(self, rank, half):
        return self.out.at[2 * rank + half]

    def whole_block(self, index):
        return False

    def start(self):
        p = self.place
        halves = [self.own.at[pl.ds(h * self.half, self.half)] for h in range(2)]
        self.kept = [
            pltpu.make_async_copy(halves[h], self.part(p.me, h), self.sem.at[0, (13, 15)[h]]) for h in range(2)
        ]
        self.go(halves[0], self.part(p.me, 0), 0, p.x)
        self.go(halves[1], self.part(p.me, 1), 3, p.y)
        self.go(halves[0], self.part(p.me, 0), 6, p.p)
        self.go(halves[1], self.part(p.me, 1), 14, p.p)
        self.go(halves[1], self.part(p.me, 1), 1, p.x)
        self.go(halves[0], self.part(p.me, 0), 2, p.y)
        for copy in self.kept:
            copy.start()

    def first_partner(self):
        for h in range(2):
            self.arrived(self.place.p, h, (6, 14)[h])
        self.met = True

    def own_in(self):
        for copy in self.kept:
            copy.wait()

    def finish(self):
        self.sent()


def packed(block):
    rows = block.shape[0] // 2
    tail = jnp.concatenate([block[:, LANES:], jnp.zeros((2 * rows, 64), block.dtype)], axis=1)
    first = lax.broadcasted_iota(jnp.int32, (rows, LANES), 1) < 64
    return jnp.concatenate([block[:, :LANES], jnp.where(first, tail[:rows], pltpu.roll(tail[rows:], 64, 1))], axis=0)


def unpacked(block):
    rows = block.shape[0] // 3
    tail = block[2 * rows :].astype(jnp.float32)
    tails = jnp.concatenate([tail, pltpu.roll(tail, 64, 1)], axis=0)[:, :64].astype(block.dtype)
    return jnp.concatenate([block[: 2 * rows], tails], axis=1)


class PlaneReduce:
    def __init__(self, place, block, recv, sem):
        self.place, self.block, self.recv, self.sem = place, block, recv, sem

    def hop(self, ok, part, slot, target, first, wait):
        copy = send(
            self.block.at[part], self.recv.at[slot], self.sem.at[0, part], self.sem.at[1, slot], fsdp=target
        )

        @pl.when(ok)
        def _():
            if wait:
                copy.wait_send()
                return
            if not first:
                self.merge(part, part)
            copy.start()

    def merge(self, part, slot):
        piece = self.recv.at[slot]
        pltpu.make_async_copy(piece, piece, self.sem.at[1, slot]).wait()
        total = self.block[part].astype(jnp.float32) + self.recv[slot].astype(jnp.float32)
        self.block[part] = total.astype(jnp.bfloat16)

    def ends(self, i, wait=False):
        z = self.place.z
        low = z == 0
        part = jnp.where(low, 3 - i, i)
        slot = part if i < 2 else jnp.where(low, part, 4)
        self.hop(jnp.logical_or(low, z == 3), part, slot, jnp.where(low, 1, 2), True, wait)

    def inner(self, up, down, slot_up, slot_down, to_up, to_down, wait=False):
        z = self.place.z
        low = z == 1
        part = jnp.where(low, up, down)
        slot = jnp.where(low, slot_up, slot_down)
        self.hop(jnp.logical_or(low, z == 2), part, slot, jnp.where(low, to_up, to_down), False, wait)

    def start(self, wait=False):
        for i in range(3):
            self.ends(i, wait)

    def step1(self, wait=False):
        self.inner(3, 0, 3, 0, 2, 1, wait)

    def step2(self, wait=False):
        self.inner(2, 1, 2, 4, 2, 1, wait)
        self.inner(0, 3, 4, 3, 0, 3, wait)

    def total(self):
        z = self.place.z

        @pl.when(z > 0)
        def _():
            self.merge(z, z)

        @pl.when(z < 3)
        def _():
            self.merge(z, 4)

    def own(self):
        return self.block.at[self.place.z]

    def finish(self):
        self.start(True)
        self.step1(True)
        self.step2(True)


class Steps:
    def __init__(self, *steps):
        self.steps = list(steps)

    def next(self, count=1):
        for step in self.steps[:count]:
            step()
        self.steps = self.steps[count:]

    def rest(self):
        self.next(len(self.steps))


class OutGather(Gather):
    def __init__(self, place, own, out, sem):
        self.place, self.own, self.out, self.sem = place, own, out, sem
        self.half = out.shape[0] // 2
        self.started = []
        self.met = False

    def part(self, rank, half):
        return self.out.at[pl.ds(half * self.half, self.half), rank]

    def whole(self, rank):
        return self.out.at[:, rank]


def front_kernel(
    tok, pos, attn_own, ffn_own, qkv_own, gu_own, far_cos, far_sin, near, out_weight, down_weight, up,
    middle_grad, gain_grad, spots, gains, down_sum,
    hidden_o, qkv_o, down_o, q_o, k_o, v_o, att_o, lse_o, middle_o, turn_o, normed, agrad, low_all, gu_out, mcols,
    hidden, qkv_w, down_w, q_ref, k_ref, v_ref, att_ref, lse_ref, middle, turn_ref, mcols_send, up_low, spot, gain_own,
    wide_in, up_all, gul, gu_w, out_block, out_w, low_sorted, gain_all, spots_s, order_s, low,
    attended, own, mine, theirs, first, out, second, down_g, down_r,
    tok_sem, up_sem, spot_sem, gain_sem, qkv_sem, out_sem, outc_sem, gu_sem, down_sem, local_sem,
    low_sem, gather_sem, reduce_sem, agrad_sem, lows_sem, down_zs, mcols_sem,
):
    place = Place()
    n = place.n
    rows = tok.shape[0]
    half = rows // 2
    pairs = 8
    heads = rows
    length = n * rows
    width = tok.shape[1]
    out_own = out_weight.at[0, pl.ds(place.me * (out_weight.shape[1] // 8), out_weight.shape[1] // 8)]
    down_own = down_weight.at[0, pl.ds(place.me * (down_weight.shape[1] // 8), down_weight.shape[1] // 8)]
    spot[...] = jnp.broadcast_to(pos[0:1, 0:1], spot.shape)
    gain_own[pl.ds(0, 1), :] = attn_own[...].astype(jnp.float32)
    gain_own[pl.ds(1, 1), :] = ffn_own[...].astype(jnp.float32)
    fetch = pltpu.make_async_copy(up, middle_grad, local_sem.at[0])
    fetch.start()
    greet(place, planes=True)
    spans = Share(place, spot, spots, spot_sem)
    scales = PlaneShare(place, gain_own, gain_all, gain_sem)
    tokens = HalfGather(place, tok, wide_in, tok_sem)
    cots = Gather(place, up_low, up_all, up_sem)
    qkvs = PlaneGather(place, qkv_own, qkv_w, qkv_sem)
    outs = PlaneGather(place, out_own, out_block, out_sem)
    outc = OutGather(place, out_block, out_w, outc_sem)
    gus = PlaneGather(place, gu_own, gu_w, gu_sem)
    downs = PlaneGather(place, down_own, down_w, down_sem)
    given = []

    def give(source, target):
        copy = pltpu.make_async_copy(source, target, local_sem.at[5 + len(given)])
        copy.start()
        given.append(copy)

    tokens.start()
    qkvs.start()
    spans.start()
    scales.start()

    def turn_rows(at, carry):
        base = near[...]
        turn_ref[at] = base * far_cos[pl.ds(at, 1), :] + pltpu.roll(base, 64, 1) * far_sin[pl.ds(at, 1), :]
        return carry

    lax.fori_loop(0, 2 * pairs, turn_rows, 0)
    give(turn_ref, turn_o)
    fetch.wait()
    up_low[...] = middle_grad[...].astype(jnp.bfloat16)
    tokens.relay()
    qkvs.step(1)
    outs.start()
    qkvs.step(2)
    tokens.rest()
    cots.start()
    outs.step(1)
    downs.start()
    qkvs.step(3)
    tokens.partner()
    tokens.own_in()
    spans.finish()
    scales.finish()
    qkvs.keep.wait()
    table = pltpu.make_async_copy(spots, spots_s, local_sem.at[1])
    table.start()
    for g in range(2):
        gains[pl.ds(g, 1), :] = jnp.concatenate([gain_all[z, pl.ds(g, 1), :] for z in range(4)], axis=1)
    table.wait()
    early = [lax.div(spots_s[j, 0, 0], half) for j in range(pairs)]
    for t in range(pairs):
        at = 0
        for j in range(pairs):
            at = jnp.where(early[j] == t, j, at)
        order_s[t] = 2 * at
        order_s[2 * pairs - 1 - t] = 2 * at + 1
    cots.relay()

    def project(j, store):
        x = jnp.concatenate([wide_in[order_s[4 * j + i]] for i in range(4)], axis=0).astype(jnp.float32)
        factor = lax.rsqrt(jnp.mean(x * x, axis=-1, keepdims=True) + epsilon)
        scaled = (x * factor * gains[pl.ds(0, 1), :]).astype(jnp.bfloat16)
        store[pl.ds(2 * (j % 2), 2)] = scaled.reshape(2, rows, -1)
        proj = nn(scaled, qkv_w[...].reshape(-1, 3 * LANES))
        spread = spread_heads(proj)
        for piece in range(4):
            at = 4 * j + piece
            cosine, sine = wave(turn_ref[at])

            def turned(part):
                z = spread[part][piece * half : (piece + 1) * half]
                return (z * cosine + pltpu.roll(z, 64, 1) * sine).astype(jnp.bfloat16)

            base = (2 * j + piece // 2) * 4 * half + (piece % 2) * half
            q_ref[pl.ds(pl.multiple_of(base, half), half), :] = turned(0)
            q_ref[pl.ds(pl.multiple_of(base + 2 * half, half), half), :] = turned(1)
            k_ref[pl.ds(pl.multiple_of(at * half, half), half), :] = turned(2)
            v_ref[pl.ds(pl.multiple_of(at * half, half), half), :] = spread[3][piece * half : (piece + 1) * half].astype(jnp.bfloat16)

    def project_first(j, carry):
        project(j, theirs)
        return carry

    def project_second(j, carry):
        project(j, first)
        return carry

    lax.fori_loop(0, 2, project_first, 0)
    keep_first = pltpu.make_async_copy(theirs, normed.at[pl.ds(0, 4)], local_sem.at[2])
    keep_first.start()
    lax.fori_loop(2, 4, project_second, 0)
    keep_second = pltpu.make_async_copy(first, normed.at[pl.ds(4, 4)], local_sem.at[3])
    keep_second.start()
    give(q_ref, q_o)
    give(k_ref, k_o)
    give(v_ref, v_o)
    give(qkv_w, qkv_o)
    tokens.finish()
    outs.step(2)
    cots.rest()
    outs.step(3)
    outs.keep.wait()
    outc.start()

    def next_weights():
        downs.step(1)
        gus.start()

    steps = Steps(next_weights, lambda: None, outc.relay, lambda: downs.step(2))
    scaling = HEAD_DIM ** (-0.5)
    lane = lax.broadcasted_iota(jnp.int32, (half, LANES), 1)
    values_t = v_ref[...].astype(jnp.float32).T.astype(jnp.bfloat16)
    def attend_group(group):
        before = group * 4 * half

        def attend(place_of, carry):
            pair = 2 * group + place_of
            q = q_ref[pl.ds(pl.multiple_of(pair * 4 * half, 4 * half), 4 * half), :]
            scores = nt(k_ref[pl.ds(before, 4 * half), :], q) * scaling
            parts = [jnp.where(causal(2 * half, place_of), scores, -1e30)]
            if group:
                parts.append(nt(k_ref[pl.ds(0, before), :], q) * scaling)
            tops = [jnp.max(part, axis=0, keepdims=True) for part in parts]
            top = jnp.maximum(tops[0], tops[-1])
            parts = [jnp.exp(part - top) for part in parts]
            total = sum(jnp.sum(part, axis=0, keepdims=True) for part in parts)
            parts = [(part * (1.0 / total)).astype(jnp.bfloat16) for part in parts]
            lse_ref[pl.ds(pair, 1), :] = top + jnp.log(total)
            out_t = nn(values_t[:, before : before + 4 * half], parts[0])
            if group:
                out_t = out_t + nn(values_t[:, :before], parts[1])
            att_ref[pl.ds(pl.multiple_of(pair * LANES, LANES), LANES), :] = out_t
            result = out_t.T.astype(jnp.bfloat16).astype(jnp.float32)
            for part in range(2):
                left = result[part * half : (part + 1) * half]
                right = pltpu.roll(result[(2 + part) * half : (3 + part) * half], half, 1)
                low_sorted[2 * pair + part, :, 0:LANES] = jnp.where(lane < half, left, right).astype(jnp.bfloat16)
                low_sorted[2 * pair + part, :, LANES:] = right.astype(jnp.bfloat16)
            return carry

        lax.fori_loop(0, 2, attend, 0)

    for group in range(pairs // 2):
        attend_group(group)
        steps.next()
    give(att_ref, att_o)
    give(lse_ref, lse_o)
    for j in range(pairs):
        upper = low_sorted[early[j]]
        lower = low_sorted[2 * pairs - 1 - early[j]]
        low[j, pl.ds(0, half), :] = upper[:, :LANES]
        low[j, pl.ds(half, half), :] = lower[:, :LANES]
        tails = jnp.where(
            lane < 64, upper[:, LANES:].astype(jnp.float32), pltpu.roll(lower[:, LANES:].astype(jnp.float32), 64, 1)
        )
        low[j, pl.ds(2 * half, half), :] = tails.astype(jnp.bfloat16)
    keep_first.wait()
    keep_second.wait()
    moved = Exchange(place, low, attended, low_sem)
    moved.start()
    outc.rest()
    outc.partner()
    cots.partner()
    outc.keep.wait()
    moved.finish()
    middle[...] = tok[...].astype(jnp.float32)

    def out_project(q, carry):
        middle[...] += nn(unpacked(attended[q]), out_w[q // 2, pl.ds(4 * (q % 2), 4)].reshape(heads, -1))
        return carry

    lax.fori_loop(0, n, out_project, 0)
    give(middle, middle_o)
    gus.step(1)
    total = middle[...]
    factor = lax.rsqrt(jnp.mean(total * total, axis=-1, keepdims=True) + epsilon)
    own[...] = (total * factor * gains[pl.ds(1, 1), :]).astype(jnp.bfloat16)
    seconds = HalfGather(place, own, wide_in, gather_sem)
    seconds.start()
    seconds.relay()
    gus.step(2)
    seconds.rest()
    lows = Gather(place, low, low_all, lows_sem)
    lows.start()
    seconds.partner()
    downs.step(3)
    downs.keep.wait()
    give(down_w, down_o)
    cots.keep.wait()
    seconds.own_in()

    def early_grad(i, carry):
        rank = flip(place, i)
        at = pl.multiple_of((i % 2) * hidden.shape[2], LANES)
        mine[i // 2, :, pl.ds(at, hidden.shape[2])] = nt(up_all[rank], down_w[...].reshape(hidden.shape[2], -1))
        return carry

    lax.fori_loop(0, n, early_grad, 0)
    gus.step(3)
    gus.keep.wait()
    grads = Reduce(place, mine, theirs, first, out, second, reduce_sem)
    wide = hidden.shape[2]

    def block(i):
        rank = flip(place, i)
        gate_up = nn(wide_in[pl.ds(2 * rank, 2)].reshape(rows, -1), gu_w[...].reshape(-1, 2 * wide))
        gate, raised = gate_up[:, :wide], gate_up[:, wide:]
        sigmoid = 1.0 / (1.0 + jnp.exp(-gate))
        silu = gate * sigmoid
        hidden[rank] = (silu * raised).astype(jnp.bfloat16)
        hidden_grad = mine[i // 2, :, pl.ds(pl.multiple_of((i % 2) * wide, LANES), wide)]
        gul[rank, :, pl.ds(0, wide)] = (hidden_grad * raised * sigmoid * (1.0 + gate * (1.0 - sigmoid))).astype(jnp.bfloat16)
        gul[rank, :, pl.ds(wide, wide)] = (hidden_grad * silu).astype(jnp.bfloat16)
        return nt(gul[rank], gu_w[...].reshape(-1, 2 * wide))

    def block_at(t, carry):
        k = lax.rem(t // 2 + 1, 4)
        value = block(2 * k + 1 - t % 2)

        @pl.when(t % 2 == 0)
        def _():
            theirs[k] = value.astype(jnp.bfloat16)
            grads.push(k)

        @pl.when(t % 2 == 1)
        def _():
            mine[k] = value

        @pl.when(t == 2)
        def _():
            lows.relay()

        @pl.when(t == 4)
        def _():
            grads.beside()

        @pl.when(t == 5)
        def _():
            lows.rest()

        @pl.when(t == 6)
        def _():
            grads.across()

        return carry

    lax.fori_loop(0, 8, block_at, 0)
    give(hidden, hidden_o)
    grads.turn()
    down_z = PlaneReduce(place, down_g, down_r, down_zs)
    piece = down_g.shape[1]

    def down_block(t, carry):
        left = hidden[:, :, pl.ds(pl.multiple_of(t * piece, piece), piece)].reshape(length, piece)
        down_g[t] = tn(left, up_all[...].reshape(length, width)).astype(jnp.bfloat16)
        return carry

    lax.fori_loop(0, 4, down_block, 0)
    down_z.start()
    seconds.finish()
    gain_grad[...] = jnp.zeros_like(gain_grad)

    def norm_back(part, second_grad):
        x = middle[part, :]
        factor = lax.rsqrt(jnp.mean(x * x, axis=-1, keepdims=True) + epsilon)
        unit = x * factor
        gain_grad[...] += jnp.sum(second_grad * unit, axis=0, keepdims=True)
        scaled = second_grad * gains[pl.ds(1, 1), :]
        inner = jnp.mean(scaled * unit, axis=-1, keepdims=True)
        grad = middle_grad[part, :] + factor * (scaled - unit * inner)
        middle_grad[part, :] = grad
        own[part, :] = grad.astype(jnp.bfloat16)

    gus.finish(kept=True)
    shard = gu_w.shape[1]

    def gu_block(t, carry):
        left = wide_in[:, :, pl.ds(pl.multiple_of(t * shard, shard), shard)].reshape(length, shard)
        gu_w[t] = tn(left, gul[...].reshape(length, 2 * wide)).astype(jnp.bfloat16)
        return carry

    lax.fori_loop(0, 4, gu_block, 0)
    give(gu_w, gu_out)
    down_z.step1()
    grads.total(norm_back)

    def head_grads(q, carry):
        weight = out_w[q // 2, pl.ds(4 * (q % 2), 4)].reshape(heads, -1)
        attended[q] = packed(nt(own[...], weight)).astype(jnp.bfloat16)
        return carry

    lax.fori_loop(0, n, head_grads, 0)
    heads_back = Exchange(place, attended, agrad, agrad_sem)
    heads_back.start()
    for q in range(8):
        mcols_send[q] = packed(own[:, q * heads : (q + 1) * heads].astype(jnp.float32)).astype(jnp.bfloat16)
    columns = Exchange(place, mcols_send, mcols, mcols_sem)
    columns.start()
    down_z.step2()
    lows.partner()
    heads_back.finish()
    down_z.total()
    down_sum[...] = down_g[place.z]
    for move in (qkvs, outs, downs, cots, outc):
        move.finish(kept=True)
    lows.finish()
    columns.finish()
    for copy in given:
        copy.wait()
    grads.finish()
    down_z.finish()


def front_moves(tok, pos, attn_own, ffn_own, qkv_own, gu_own, far_cos, far_sin, near, out_weight, down_weight, up):
    n, planes = lax.axis_size("ctx"), lax.axis_size("fsdp")
    rows, width = tok.shape
    length = n * rows
    bf, f32 = jnp.bfloat16, jnp.float32
    shape = jax.ShapeDtypeStruct
    out_own = shape((out_weight.shape[1] // n, width), bf)
    down_own = shape((down_weight.shape[1] // n, width), bf)
    spot = shape((8, LANES), jnp.int32)
    gain_own = shape((8, attn_own.shape[1]), f32)
    wide = planes * down_own.shape[0]
    dma = pltpu.SemaphoreType.DMA
    pairs = length // 192
    halves = pltpu.VMEM((6, rows // 2, width), bf)
    quads = pltpu.VMEM((4, rows, width), bf)
    small = (n, 3 * rows // 2, LANES)
    all_of = lambda x: shape((planes,) + x.shape, x.dtype)
    gathered = lambda x: pltpu.VMEM((planes,) + x.shape, x.dtype)
    ring = dma((2, Gather.sems))
    half_ring = dma((2, HalfGather.sems))
    line = dma((3, planes))
    swap = dma((2, n))
    kept = (
        shape((n, rows, wide), bf), all_of(qkv_own), all_of(down_own),
        shape((2 * length, LANES), bf), shape((length, LANES), bf), shape((length, LANES), bf),
        shape((pairs * LANES, 384), f32), shape((pairs, 384), f32), shape((rows, width), f32),
        shape((2 * n, rows // 2, LANES), f32),
    )
    return pl.pallas_call(
        front_kernel,
        out_shape=(
            shape((rows, width), f32), shape((1, width), f32), shape((n,) + spot.shape, spot.dtype), shape((2, width), f32),
            shape(down_own.shape, bf),
        ) + kept + (shape((n, rows, width), bf), shape(small, bf), shape((n,) + small, bf), all_of(gu_own), shape(small, bf)),
        in_specs=vm(9) + anywhere(3),
        out_specs=vm(5) + anywhere(15),
        scratch_shapes=[pltpu.VMEM(x.shape, x.dtype) for x in kept] + [
            pltpu.VMEM(small, bf), pltpu.VMEM((rows, width), bf), pltpu.VMEM(spot.shape, jnp.int32), pltpu.VMEM(gain_own.shape, f32),
            pltpu.VMEM((2 * n, rows // 2, width), bf), pltpu.VMEM((n, rows, width), bf), pltpu.VMEM((n, rows, 2 * wide), bf),
            gathered(gu_own), gathered(out_own), pltpu.VMEM((planes, n) + out_own.shape, bf),
            pltpu.VMEM((16, 96, 2 * LANES), bf), gathered(gain_own), pltpu.SMEM((n,) + spot.shape, jnp.int32),
            pltpu.SMEM((2 * n,), jnp.int32), pltpu.VMEM(small, bf),
            pltpu.VMEM(small, bf), pltpu.VMEM((rows, width), bf),
            pltpu.VMEM((4, rows, width), f32), quads, quads, halves, halves,
            gathered(down_own), pltpu.VMEM((planes + 1,) + down_own.shape, bf),
            half_ring, ring, swap, dma((2, planes)), line, line, ring, line, line, dma((16,)),
            swap, half_ring, dma((2, Reduce.sems)), swap, ring, dma((2, planes + 1)), swap,
        ],
        compiler_params=pltpu.CompilerParams(collective_id=1, has_side_effects=True, vmem_limit_bytes=67043328),
        name="front_moves",
    )(tok, pos, attn_own, ffn_own, qkv_own, gu_own, far_cos, far_sin, near, out_weight, down_weight, up)


def back_moves_kernel(
    tok, gain, ffn_gain, down_sum, spots_i,
    gu_i, middle_grad_i, hidden_i, down_i, k_i, q_i, v_i, agrad_i, att_i, lse_i, turn_i, normed_i, middle_i, qkv_i, mcols_i, low_i,
    grad, result, attn_sum, ffn_sum, down_all, gu_all, out_all, qkv_all,
    spots_s, agrad_at, gu_g, hidden, down_w, k_ref, q_ref, v_ref, agrad, att_ref, lse_ref, turn_ref, normed_in, middle, qkv_w, mcols_in, low_in, out_g, qkv_g, gu_r, out_r, qkv_r,
    mine, theirs, first, out, second, dk_ref, dv_ref, pg_sorted, mcols,
    gain_sum, mine_gain, ctx_gain, plane_sum, plane_gain,
    free, local_sem, sum_sem, reduce_sem, gu_zs, out_zs, qkv_zs, down_cs, gu_cs, out_cs, qkv_cs,
    gain_sem, plane_sem,
):
    place = Place()
    n = place.n
    rows = tok.shape[0]
    half = rows // 2
    pairs = 8
    width = tok.shape[1]
    length = n * rows
    loads = [
        pltpu.make_async_copy(source, target, local_sem.at[at])
        for at, (source, target) in enumerate((
            (gu_i, gu_g), (hidden_i, hidden), (down_i, down_w), (k_i, k_ref), (q_i, q_ref), (v_i, v_ref),
            (agrad_i, agrad), (att_i, att_ref), (lse_i, lse_ref), (turn_i, turn_ref), (middle_i, middle),
            (normed_i, normed_in), (qkv_i, qkv_w), (mcols_i, mcols_in), (low_i, low_in), (middle_grad_i, grad),
        ))
    ]
    table = pltpu.make_async_copy(spots_i, spots_s, local_sem.at[16])
    table.start()
    for load in loads:
        load.start()
    greet(place, planes=True)
    table.wait()
    early = [lax.div(spots_s[j, 0, 0], half) for j in range(pairs)]
    holder = []
    for t in range(pairs):
        at = 0
        for j in range(pairs):
            at = jnp.where(early[j] == t, j, at)
        holder.append(at)
    gu_z = PlaneReduce(place, gu_g, gu_r, gu_zs)
    out_z = PlaneReduce(place, out_g, out_r, out_zs)
    qkv_z = PlaneReduce(place, qkv_g, qkv_r, qkv_zs)
    sums = Reduce(place, mine, theirs, first, out, second, sum_sem)
    downs = Gather(place, down_sum, down_all, down_cs)
    gus = Gather(place, gu_z.own(), gu_all, gu_cs)
    loads[0].wait()
    gu_z.start()
    downs.start()
    loads[1].wait()
    loads[2].wait()

    def other(k, carry):
        theirs[k] = nn(hidden[flip(place, 2 * k + 1)], down_w[...].reshape(-1, width)).astype(jnp.bfloat16)
        sums.push(k)
        return carry

    def ours(k, carry):
        mine[k] = nn(hidden[flip(place, 2 * k)], down_w[...].reshape(-1, width))
        return carry

    lax.fori_loop(0, 4, other, 0)
    lax.fori_loop(0, 4, ours, 0)
    downs.relay()
    sums.across()
    sums.beside()
    for load in loads[3:11]:
        load.wait()

    def finish_rows(part, down_out):
        result[part, :] = (middle[part, :] + down_out).astype(jnp.bfloat16)

    def sums_done():
        sums.total(finish_rows)
        sums.finish()
        for rank in (place.p, place.x, place.y):
            pl.semaphore_signal(free, inc=1, device_id={"ctx": rank}, device_id_type=MESH)

    def columns_done():
        loads[13].wait()

        def unpack(q, carry):
            mcols[q] = unpacked(mcols_in[q])
            return carry

        lax.fori_loop(0, n, unpack, 0)

    steps = Steps(downs.rest, gu_z.step1, lambda: (downs.partner(), sums.turn()), columns_done)
    scaling = HEAD_DIM ** (-0.5)
    lane = lax.broadcasted_iota(jnp.int32, (half, LANES), 1)
    keys_t = k_ref[...].astype(jnp.float32).T.astype(jnp.bfloat16)
    ranks_s = agrad_at
    for t in range(pairs):
        ranks_s[t] = holder[t]
        ranks_s[2 * pairs - 1 - t] = holder[t]
    dk_ref[...] = jnp.zeros_like(dk_ref)
    dv_ref[...] = jnp.zeros_like(dv_ref)

    def back_group(group):
        before = group * 4 * half
        side = 0 if group < pairs // 4 else 1
        cuts = [(before, 4 * half)] + [(at, min(768, before - at)) for at in range(0, before, 768)]

        def back(place_of, carry):
            pair = 2 * group + place_of
            q = q_ref[pl.ds(pl.multiple_of(pair * 4 * half, 4 * half), 4 * half), :]
            firsts, seconds = [], []
            for part in range(2):
                piece_of = agrad[ranks_s[2 * pair + part]].astype(jnp.float32)
                left = piece_of[side * half : (side + 1) * half]
                tail = piece_of[2 * half :]
                right = tail if side == 0 else pltpu.roll(tail, 64, 1)
                firsts.append(jnp.where(lane < half, left, 0.0))
                seconds.append(
                    jnp.where(lane < half, pltpu.roll(jnp.where(lane < half, right, left), LANES - half, 1), 0.0)
                )
            grads = jnp.concatenate(firsts + seconds, axis=0)
            att_t = att_ref[pl.ds(pl.multiple_of(pair * LANES, LANES), LANES), :]
            delta = jnp.sum(grads.T * att_t, axis=0, keepdims=True)
            grads = grads.astype(jnp.bfloat16)
            dq_t = None
            for at, count in cuts:
                keys = pl.ds(at, count)
                weights = jnp.exp(
                    jnp.where(
                        causal(2 * half, place_of), nt(k_ref[keys, :], q) * scaling - lse_ref[pl.ds(pair, 1), :], -1e30
                    )
                    if at == before
                    else nt(k_ref[keys, :], q) * scaling - lse_ref[pl.ds(pair, 1), :]
                )
                dp = nt(v_ref[keys, :], grads)
                ds = (weights * (dp - delta)).astype(jnp.bfloat16)
                dk_ref[keys, :] += nn(ds, q) * scaling
                dv_ref[keys, :] += nn(weights.astype(jnp.bfloat16), grads)
                term = nn(keys_t[:, at : at + count], ds)
                dq_t = term if dq_t is None else dq_t + term
            dq = dq_t.T * scaling
            for part in range(2):
                cosine, sine = wave(turn_ref[2 * pair + part])
                turned = []
                for head in range(2):
                    z = dq[(2 * head + part) * half : (2 * head + part + 1) * half]
                    turned.append(close_halves(z * cosine - pltpu.roll(z, 64, 1) * sine))
                second_head = pltpu.roll(turned[1], 96, 1)
                pg_sorted[2 * pair + part, :, 0:LANES] = jnp.where(lane < 96, turned[0], second_head).astype(jnp.bfloat16)
                pg_sorted[2 * pair + part, :, LANES : 2 * LANES] = second_head.astype(jnp.bfloat16)
            return carry

        lax.fori_loop(0, 2, back, 0)

    for group in reversed(range(pairs // 2)):
        back_group(group)
        steps.next()
    for s in range(2 * pairs):
        spot = pl.ds(s * half, half)
        cosine, sine = wave(turn_ref[s])
        z = dk_ref[spot, :]
        key_head = pltpu.roll(close_halves(z * cosine - pltpu.roll(z, 64, 1) * sine), 64, 1)
        queries_too = pg_sorted[s, :, LANES : 2 * LANES].astype(jnp.float32)
        pg_sorted[s, :, LANES : 2 * LANES] = jnp.where(lane < 64, queries_too, key_head).astype(jnp.bfloat16)
        pg_sorted[s, :, 2 * LANES :] = jnp.where(lane < 32, key_head, pltpu.roll(dv_ref[spot, :], 32, 1)).astype(jnp.bfloat16)

    loads[11].wait()
    loads[12].wait()
    shard = gu_g.shape[1]

    def qkv_block(t, carry):
        left = normed_in[:, :, pl.ds(pl.multiple_of(t * shard, shard), shard)].reshape(length, shard)
        qkv_g[t] = tn(left, pg_sorted[...].reshape(length, 3 * LANES)).astype(jnp.bfloat16)
        return carry

    sums_done()
    lax.fori_loop(0, 4, qkv_block, 0)
    qkv_z.start()
    gu_z.step2()
    pl.semaphore_wait(free, 3)
    grads = Reduce(place, mine, theirs, first, out, second, reduce_sem)

    def chunk(i):
        at = lax.div(spots_s[flip(place, i), 0, 0], half)
        rows_of = jnp.concatenate([pg_sorted[at], pg_sorted[2 * pairs - 1 - at]], axis=0)
        return nt(rows_of, qkv_w[...].reshape(width, -1))

    def push(k, carry):
        theirs[k] = chunk(2 * k + 1).astype(jnp.bfloat16)
        grads.push(k)
        return carry

    def keep(k, carry):
        mine[k] = chunk(2 * k)
        return carry

    lax.fori_loop(0, 4, push, 0)
    lax.fori_loop(0, 4, keep, 0)
    grads.across()
    grads.beside()
    loads[14].wait()
    loads[15].wait()

    def out_block(src, carry):
        heads = low_in[src, :, pl.ds(0, rows), :].reshape(length, LANES)
        tails = low_in[src, :, pl.ds(rows, half), :].reshape(length // 2, LANES)
        upper = tn(heads, mcols[...].reshape(length, rows))
        from_a = tn(tails, mcols[:, pl.ds(0, half), :].reshape(length // 2, rows))
        from_b = tn(tails, mcols[:, pl.ds(half, half), :].reshape(length // 2, rows))
        at = pl.multiple_of((src % 2) * rows, rows)
        out_g[src // 2, pl.ds(at, LANES), :] = upper.astype(jnp.bfloat16)
        out_g[src // 2, pl.ds(pl.multiple_of(at + LANES, 64), 64), :] = (from_a[:64] + from_b[64:]).astype(jnp.bfloat16)
        return carry

    lax.fori_loop(0, 8, out_block, 0)
    out_z.start()
    grads.turn()
    gu_z.total()
    gus.start()
    gain_sum[...] = jnp.zeros_like(gain_sum)

    def norm_back(part, normed_grad):
        x = tok[part, :].astype(jnp.float32)
        factor = lax.rsqrt(jnp.mean(x * x, axis=-1, keepdims=True) + epsilon)
        unit = x * factor
        gain_sum[...] += jnp.sum(normed_grad * unit, axis=0, keepdims=True)
        scaled = normed_grad * gain[pl.ds(0, 1), :]
        inner = jnp.mean(scaled * unit, axis=-1, keepdims=True)
        grad[part, :] = grad[part, :] + factor * (scaled - unit * inner)

    qkv_z.step1()
    grads.total(norm_back)
    gain_grad = gain_sum[...]
    count = mine_gain.shape[0] // 2
    for at in range(count):
        mine_gain[pl.ds(at, 1), :] = gain_grad[:, at * shard : (at + 1) * shard]
        mine_gain[pl.ds(count + at, 1), :] = ffn_gain[:, at * shard : (at + 1) * shard]
    ctx_sum = Share(place, mine_gain, ctx_gain, gain_sem)
    ctx_sum.start()
    gus.relay()
    qkv_z.step2()
    out_z.step1()
    ctx_sum.finish()
    plane_sum[...] = jnp.sum(ctx_gain[...], axis=0)
    planes = PlaneShare(place, plane_sum, plane_gain, plane_sem)
    planes.start()
    out_z.step2()
    qkv_z.total()
    gus.rest()
    qkvs = Gather(place, qkv_z.own(), qkv_all, qkv_cs)
    qkvs.start()
    out_z.total()
    outs = Gather(place, out_z.own(), out_all, out_cs)
    qkvs.relay()
    outs.start()
    qkvs.rest()
    outs.relay()
    outs.rest()
    planes.finish()
    plane_sum[...] = jnp.sum(plane_gain[...], axis=0)
    attn_sum[...] = plane_sum[pl.ds(place.z, 1), :]
    ffn_sum[...] = plane_sum[pl.ds(count + place.z, 1), :]
    gus.partner()
    qkvs.partner()
    outs.partner()
    for move in (gu_z, out_z, qkv_z, downs, gus, outs, qkvs, grads):
        move.finish()


def back_moves(tok, gain, ffn_gain, down_sum, spots, *moved):
    n, planes = lax.axis_size("ctx"), lax.axis_size("fsdp")
    rows, width = tok.shape
    length = n * rows
    shard = width // planes
    bf, f32 = jnp.bfloat16, jnp.float32
    shape = jax.ShapeDtypeStruct
    dma = pltpu.SemaphoreType.DMA
    halves = pltpu.VMEM((6, rows // 2, width), bf)
    quads = pltpu.VMEM((4, rows, width), bf)
    small = (2 * planes, shard)
    parts = (moved[0].shape[1:], (shard, rows), (shard, 3 * LANES))
    ring = dma((2, Gather.sems))
    return pl.pallas_call(
        back_moves_kernel,
        out_shape=(shape((rows, width), f32), shape((rows, width), bf), shape((1, shard), f32), shape((1, shard), f32))
        + tuple(shape((n,) + part, bf) for part in (down_sum.shape,) + parts),
        in_specs=vm(4) + anywhere(1 + len(moved)),
        out_specs=vm(4) + anywhere(4),
        scratch_shapes=[pltpu.SMEM(spots.shape, jnp.int32), pltpu.SMEM((2 * n,), jnp.int32)] + [pltpu.VMEM(x.shape, x.dtype) for at, x in enumerate(moved) if at != 1]
        + [pltpu.VMEM((planes,) + part, bf) for part in parts[1:]]
        + [pltpu.VMEM((planes + 1,) + part, bf) for part in parts]
        + [
            pltpu.VMEM((4, rows, width), f32), quads, quads, halves, halves,
            pltpu.VMEM((length, LANES), f32), pltpu.VMEM((length, LANES), f32), pltpu.VMEM((16, 96, 3 * LANES), bf),
            pltpu.VMEM((n, rows, rows), bf),
            pltpu.VMEM((1, width), f32), pltpu.VMEM(small, f32), pltpu.VMEM((n,) + small, f32),
            pltpu.VMEM(small, f32), pltpu.VMEM((planes,) + small, f32),
            pltpu.SemaphoreType.REGULAR, dma((17,)), dma((2, Reduce.sems)), dma((2, Reduce.sems)),
            dma((2, 5)), dma((2, 5)), dma((2, 5)), ring, ring, ring, ring, dma((2, n)), dma((2, planes)),
        ],
        compiler_params=pltpu.CompilerParams(collective_id=6, has_side_effects=True, vmem_limit_bytes=67043328),
        name="back_moves",
    )(tok, gain, ffn_gain, down_sum, spots, *moved)


def pack_kernel(
    down, gu, out, qkv, grad, result, attn, ffn, down_o, gu_o, out_o, qkv_o, grad_o, result_o, attn_o, ffn_o
):
    devices, rows = gu.shape[0], gu.shape[1]
    f32 = jnp.float32
    lane = lax.broadcasted_iota(jnp.int32, (rows, LANES), 1)
    down_o[...] = down[0].astype(f32)
    grad_o[...] = grad[...]
    result_o[...] = result[...]
    attn_o[...] = attn[...]
    ffn_o[...] = ffn[...]
    tiles = gu_o.shape[0] // rows
    spans = gu.shape[2] // (2 * LANES)
    for r in range(0, rows, 16):
        pieces = [
            gu[c, pl.ds(r, 16), (s * spans + z) * LANES : (s * spans + z + 1) * LANES].astype(f32)
            for z in range(spans) for c in range(devices) for s in range(2)
        ]
        gu_o[pl.ds(r * tiles, 16 * tiles), :] = jnp.swapaxes(jnp.stack(pieces, axis=0), 0, 1).reshape(16 * tiles, LANES)

    def tile(c, at):
        return qkv[c, :, at * LANES : (at + 1) * LANES].astype(f32)

    def key_head(c):
        return jnp.where(lane < 64, pltpu.roll(tile(c, 1), 64, 1), pltpu.roll(tile(c, 2), 64, 1))

    def value_head(c):
        return pltpu.roll(tile(c, 2), 96, 1)

    def store(at, heads):
        second, third, fourth = pltpu.roll(heads[1], 96, 1), pltpu.roll(heads[2], 64, 1), pltpu.roll(heads[3], 32, 1)
        qkv_o[:, at : at + LANES] = jnp.where(lane < 96, heads[0], second)
        qkv_o[:, at + LANES : at + 2 * LANES] = jnp.where(lane < 64, second, third)
        qkv_o[:, at + 2 * LANES : at + 3 * LANES] = jnp.where(lane < 32, third, fourth)

    for c in range(0, devices, 2):
        at = c * 192
        turned = pltpu.roll(tile(c + 1, 0), 64, 1)
        qkv_o[:, at : at + LANES] = tile(c, 0)
        qkv_o[:, at + LANES : at + 2 * LANES] = jnp.where(lane < 64, tile(c, 1), turned)
        qkv_o[:, at + 2 * LANES : at + 3 * LANES] = jnp.where(lane < 64, turned, pltpu.roll(tile(c + 1, 1), 64, 1))
    for c in range(0, devices, 4):
        store(HEADS * HEAD_DIM + c * 96, [key_head(c + i) for i in range(4)])
        store((HEADS + KV_HEADS) * HEAD_DIM + c * 96, [value_head(c + i) for i in range(4)])
    for c in range(0, devices, 2):
        at = c * 192
        first = out[c].astype(f32)
        second = out[c + 1].astype(f32)
        tail = jnp.concatenate([first[:, LANES:], jnp.zeros((rows, 64), f32)], axis=1)
        next_tail = jnp.concatenate([second[:, LANES:], jnp.zeros((rows, 64), f32)], axis=1)
        turned = pltpu.roll(second[:, :LANES], 64, 1)
        out_o[:, at : at + LANES] = first[:, :LANES]
        out_o[:, at + LANES : at + 2 * LANES] = jnp.where(lane < 64, tail, turned)
        out_o[:, at + 2 * LANES : at + 3 * LANES] = jnp.where(lane < 64, turned, pltpu.roll(next_tail, 64, 1))


def pack(down, gu, out, qkv, grad, result, attn, ffn):
    n, shard = gu.shape[0], gu.shape[1]
    rows = shard // n
    width = down.shape[2]
    f32 = jnp.float32
    spec = pl.BlockSpec
    shape = jax.ShapeDtypeStruct
    tiles = n * gu.shape[2] // LANES
    quarter = grad.shape[0] // 4
    return pl.pallas_call(
        pack_kernel,
        grid=(n,),
        out_shape=(
            shape((n * down.shape[1], width), f32), shape((shard * tiles, LANES), f32), shape((shard, n * out.shape[2]), f32),
            shape((shard, (HEADS + 2 * KV_HEADS) * HEAD_DIM), f32), shape(grad.shape, f32), shape(result.shape, result.dtype), shape(attn.shape, f32), shape(ffn.shape, f32),
        ),
        in_specs=[
            spec((1,) + down.shape[1:], lambda i: (i, 0, 0)), spec((n, rows, gu.shape[2]), lambda i: (0, i, 0)),
            spec((n, rows, out.shape[2]), lambda i: (0, i, 0)), spec((n, rows, qkv.shape[2]), lambda i: (0, i, 0)),
            spec((quarter, width), lambda i: (i // 2, 0)), spec((quarter, width), lambda i: (i // 2, 0)),
            spec(attn.shape, lambda i: (0, 0)), spec(ffn.shape, lambda i: (0, 0)),
        ],
        out_specs=[
            spec((down.shape[1], width), lambda i: (i, 0)), spec((rows * tiles, LANES), lambda i: (i, 0)),
            spec((rows, n * out.shape[2]), lambda i: (i, 0)), spec((rows, (HEADS + 2 * KV_HEADS) * HEAD_DIM), lambda i: (i, 0)),
            spec((quarter, width), lambda i: (i // 2, 0)), spec((quarter, width), lambda i: (i // 2, 0)),
            spec(attn.shape, lambda i: (0, 0)), spec(ffn.shape, lambda i: (0, 0)),
        ],
        name="pack",
    )(down, gu, out, qkv, grad, result, attn, ffn)


def fast_body(
    tokens, positions, qkv_weight, out_weight, gate_up_weight, down_weight, attn_gain, ffn_gain, cotangent
):
    me = lax.axis_index("ctx")
    n = lax.axis_size("ctx")
    planes = lax.axis_size("fsdp")
    rows = tokens.shape[1]
    length = n * rows
    width = tokens.shape[2]
    wide = down_weight.shape[1] * planes
    own = wide // n
    piece = own // planes
    shard = qkv_weight.shape[1]
    query_width = HEADS * HEAD_DIM
    key_width = KV_HEADS * HEAD_DIM
    cut = lax.dynamic_slice_in_dim

    qkv = qkv_weight[0]
    q_part = cut(qkv, me * 2 * HEAD_DIM, 2 * HEAD_DIM, 1)
    k_part = cut(qkv, query_width + me * HEAD_DIM, HEAD_DIM, 1)
    v_part = cut(qkv, query_width + key_width + me * HEAD_DIM, HEAD_DIM, 1)
    qkv_own = jnp.concatenate([q_part, k_part, v_part], axis=1)
    pieces = [cut(gate_up_weight[0], at * (wide // planes) + me * piece, piece, 2) for at in range(planes)]
    gate_up_own = jnp.concatenate([x[:, s] for s in range(2) for x in pieces], axis=1)
    (
        middle_grad, ffn_partial, spots, gains, down_sum, hidden, qkv_block, down_block, q, k, v, att, lse, middle,
        turns, normed, attended_grad, low_all, gate_up_grad, middle_cols,
    ) = front_moves(
        tokens[0], positions, attn_gain, ffn_gain, qkv_own, gate_up_own, *turn_parts(2 * n, rows // 2),
        out_weight, down_weight, cotangent[0],
    )
    stream_grad, result, attn_sum, ffn_sum, down_grad, gate_up_grad, out_grad, qkv_grad = back_moves(
        tokens[0], gains, ffn_partial, down_sum, spots,
        gate_up_grad, middle_grad, hidden, down_block, k, q, v, attended_grad, att, lse, turns, normed, middle,
        qkv_block, middle_cols, low_all,
    )
    down_grad, gate_up_grad, out_grad, qkv_grad, stream_grad, result, attn_sum, ffn_sum = pack(
        down_grad, gate_up_grad, out_grad, qkv_grad, stream_grad, result, attn_sum, ffn_sum
    )
    gate_up_grad = gate_up_grad.reshape(shard, wide // LANES, 2, LANES).transpose(0, 2, 1, 3).reshape(shard, 2, wide)
    return (
        result[None],
        stream_grad[None],
        qkv_grad[None],
        out_grad[None],
        gate_up_grad[None],
        down_grad[None],
        attn_sum,
        ffn_sum,
    )


def solution(mesh):
    split = mesh.shape["ctx"] == KV_HEADS and mesh.shape["fsdp"] == 4
    placed = (
        P("fsdp", "ctx", None),
        P("fsdp", "ctx"),
        P(None, "fsdp", None),
        P(None, "fsdp", None),
        P(None, "fsdp", None, None),
        P(None, "fsdp", None),
        P(None, "fsdp"),
        P(None, "fsdp"),
        P("fsdp", "ctx", None),
    )
    return jax.shard_map(
        fast_body if split else body,
        mesh=mesh,
        in_specs=placed,
        out_specs=(
            P("fsdp", "ctx", None),
            P("fsdp", "ctx", None),
            P(None, "fsdp", None),
            P(None, "fsdp", None),
            P(None, "fsdp", None, None),
            P(None, "fsdp", None),
            P(None, "fsdp"),
            P(None, "fsdp"),
        ),
        check_vma=False,
    )
```

profile of v0, /device:TPU:0, one launch (start us, length us, event | category | flops | bytes accessed | tf_op | source)
XLA Modules:
  0.0 322.5 jit_solution(16455109854287283359)
XLA Ops:
  0.6 1.2 dynamic-slice_bitcast_fusion.2
  1.8 1.1 dynamic-slice_bitcast_fusion
  2.9 0.9 pad_maximum_fusion.qkv_own
  3.8 1.8 constant_dynamic-slice_fusion
  5.6 0.1 copy_bitcast_fusion
  5.6 0.1 copy_bitcast_fusion.2
  5.7 0.6 fusion.7
  6.3 0.6 fusion.6
  7.0 0.6 fusion.5
  7.6 0.6 fusion.4
  8.3 0.6 fusion.3
  8.9 0.6 fusion.2
  9.6 0.6 fusion.1
  10.2 0.6 fusion.gu_own
  10.9 177.1 %front_moves.1 = (f32[192,1536]{1,0:T(8,128)}, f32[1,1536]{1,0:T(1,128)}, s32[8,8,128]{2,1,0:T(8,128)}, f32[2,1536]{1,0:T(2,128)}, bf16[128,1536]{1,0:T(8,128)(2...) custom-call(bf16[192,1536]{1,0:T(8,128)(2,1)} %bitcast.58, ...), custom_call_target="tpu_custom_call" | custom-call | tf_op jit(solution)/shard_map/front_moves/pallas_call | solution.py:1389
  188.0 117.0 %back_moves.1 = (f32[192,1536]{1,0:T(8,128)}, bf16[192,1536]{1,0:T(8,128)(2,1)}, f32[1,384]{1,0:T(1,128)}, f32[1,384]{1,0:T(1,128)}, bf16[8,128,1536]{2,1,0:T(8,...) custom-call(bf16[192,1536]{1,0:T(8,128)(2,1)} %bitcast.59, ...), custom_call_target="tpu_custom_call" | custom-call | tf_op jit(solution)/shard_map/back_moves/pallas_call | solution.py:1690
  304.9 17.3 %pack.1 = (f32[1024,1536]{1,0:T(8,128)}, f32[24576,128]{1,0:T(8,128)}, f32[384,1536]{1,0:T(8,128)}, f32[384,3072]{1,0:T(8,128)}, f32[192,1536]{1,0:T(8,128)}, /*...) custom-call(bf16[8,128,1536]{2,1,0:T(8,128)(2,1)} %get-tuple-element.64.down, ...), custom_call_target="tpu_custom_call" | custom-call | tf_op jit(solution)/shard_map/pack/pallas_call | solution.py:1778
where the time goes:
time: 323 us; the launch traced here: 322 us
  Pallas kernels  311 us (96%)
  local copies, waits for them, and re-layouts  9.34 us (3%)
    pallas_call x1, Pallas kernels, front_moves(): pl.pallas_call(front_kernel, out_shape=(shape((rows, width), f32), shape(...  177 us
    pallas_call x1, Pallas kernels, back_moves(): pl.pallas_call(back_moves_kernel, out_shape=(shape((rows, width), f32), s...  117 us
    pallas_call x1, Pallas kernels, pack(): pl.pallas_call(pack_kernel, grid=(n,), out_shape=(shape((n * down.shape[1...  17.3 us

commit v1 on v0

--- a/solution.py
+++ b/solution.py
@@ -1133,7 +1133,7 @@
         return carry
 
     lax.fori_loop(0, 2, project_first, 0)
-    keep_first = pltpu.make_async_copy(theirs, normed.at[pl.ds(0, 4)], local_sem.at[2])
+    keep_first = pltpu.make_async_copy(theirs.at[pl.ds(0, 4)], normed.at[pl.ds(0, 4)], local_sem.at[2])
     keep_first.start()
     lax.fori_loop(2, 4, project_second, 0)
     keep_second = pltpu.make_async_copy(first, normed.at[pl.ds(4, 4)], local_sem.at[3])
@@ -1264,14 +1264,13 @@
         k = lax.rem(t // 2 + 1, 4)
         value = block(2 * k + 1 - t % 2)
 
+        odd = t % 2
+        theirs[k * (1 - odd) + 4 * odd] = value.astype(jnp.bfloat16)
+        mine[k * odd + 4 * (1 - odd)] = value
+
         @pl.when(t % 2 == 0)
         def _():
-            theirs[k] = value.astype(jnp.bfloat16)
             grads.push(k)
-
-        @pl.when(t % 2 == 1)
-        def _():
-            mine[k] = value
 
         @pl.when(t == 2)
         def _():
@@ -1293,7 +1292,6 @@
 
     lax.fori_loop(0, 8, block_at, 0)
     give(hidden, hidden_o)
-    grads.turn()
     down_z = PlaneReduce(place, down_g, down_r, down_zs)
     piece = down_g.shape[1]
 
@@ -1304,6 +1302,7 @@
 
     lax.fori_loop(0, 4, down_block, 0)
     down_z.start()
+    grads.turn()
     seconds.finish()
     gain_grad[...] = jnp.zeros_like(gain_grad)
 
@@ -1401,7 +1400,7 @@
             pltpu.VMEM((16, 96, 2 * LANES), bf), gathered(gain_own), pltpu.SMEM((n,) + spot.shape, jnp.int32),
             pltpu.SMEM((2 * n,), jnp.int32), pltpu.VMEM(small, bf),
             pltpu.VMEM(small, bf), pltpu.VMEM((rows, width), bf),
-            pltpu.VMEM((4, rows, width), f32), quads, quads, halves, halves,
+            pltpu.VMEM((5, rows, width), f32), pltpu.VMEM((5, rows, width), bf), quads, halves, halves,
             gathered(down_own), pltpu.VMEM((planes + 1,) + down_own.shape, bf),
             half_ring, ring, swap, dma((2, planes)), line, line, ring, line, line, dma((16,)),
             swap, half_ring, dma((2, Reduce.sems)), swap, ring, dma((2, planes + 1)), swap,
@@ -1821,7 +1820,7 @@
     v_part = cut(qkv, query_width + key_width + me * HEAD_DIM, HEAD_DIM, 1)
     qkv_own = jnp.concatenate([q_part, k_part, v_part], axis=1)
     pieces = [cut(gate_up_weight[0], at * (wide // planes) + me * piece, piece, 2) for at in range(planes)]
-    gate_up_own = jnp.concatenate([x[:, s] for s in range(2) for x in pieces], axis=1)
+    gate_up_own = jnp.concatenate(pieces, axis=2).reshape(shard, 2 * own)
     (
         middle_grad, ffn_partial, spots, gains, down_sum, hidden, qkv_block, down_block, q, k, v, att, lse, middle,
         turns, normed, attended_grad, low_all, gate_up_grad, middle_cols,

time: 323 us -> 315 us (0.975)
  local copies, waits for them, and re-layouts: 9.34 us -> 5.07 us
  Pallas kernels: 311 us -> 307 us
    unnamed x7 -> x1, local copies, waits for them, and re-layouts: 4.53 us -> 1.02 us
    pallas_call x1, Pallas kernels: 177 us -> 174 us  [front_moves(): pl.pallas_call(front_kernel, out_shape=(shape((rows, width), f32), shape(...]
where the time goes in v1:
time: 315 us; the launch traced here: 314 us
  Pallas kernels  307 us (97%)
  local copies, waits for them, and re-layouts  5.07 us (2%)
    pallas_call x1, Pallas kernels, front_moves(): pl.pallas_call(front_kernel, out_shape=(shape((rows, width), f32), shape(...  174 us
    pallas_call x1, Pallas kernels, back_moves(): pl.pallas_call(back_moves_kernel, out_shape=(shape((rows, width), f32), s...  115 us
    pallas_call x1, Pallas kernels, pack(): pl.pallas_call(pack_kernel, grid=(n,), out_shape=(shape((n * down.shape[1...  17.3 us

profile of v1, /device:TPU:0, one launch (start us, length us, event | category | flops | bytes accessed | tf_op | source)
XLA Modules:
  0.0 314.3 jit_solution(4720495997309041466)
XLA Ops:
  0.6 1.2 dynamic-slice_bitcast_fusion.6
  1.8 1.1 dynamic-slice_bitcast_fusion.4
  2.9 0.9 pad_maximum_fusion.1.qkv_own
  3.8 1.8 dynamic-slice_bitcast_fusion.3
  5.6 1.0 pad_maximum_fusion
  6.6 1.0 copy.21
  7.6 173.7 %front_moves.1 = (f32[192,1536]{1,0:T(8,128)}, f32[1,1536]{1,0:T(1,128)}, s32[8,8,128]{2,1,0:T(8,128)}, f32[2,1536]{1,0:T(2,128)}, bf16[128,1536]{1,0:T(8,128)(2...) custom-call(bf16[192,1536]{1,0:T(8,128)(2,1)} %bitcast.30, ...), custom_call_target="tpu_custom_call" | custom-call | tf_op jit(solution)/shard_map/front_moves/pallas_call | solution.py:1388
  181.3 115.4 %back_moves.1 = (f32[192,1536]{1,0:T(8,128)}, bf16[192,1536]{1,0:T(8,128)(2,1)}, f32[1,384]{1,0:T(1,128)}, f32[1,384]{1,0:T(1,128)}, bf16[8,128,1536]{2,1,0:T(8,...) custom-call(bf16[192,1536]{1,0:T(8,128)(2,1)} %bitcast.31, ...), custom_call_target="tpu_custom_call" | custom-call | tf_op jit(solution)/shard_map/back_moves/pallas_call | solution.py:1689
  296.8 17.3 %pack.1 = (f32[1024,1536]{1,0:T(8,128)}, f32[24576,128]{1,0:T(8,128)}, f32[384,1536]{1,0:T(8,128)}, f32[384,3072]{1,0:T(8,128)}, f32[192,1536]{1,0:T(8,128)}, /*...) custom-call(bf16[8,128,1536]{2,1,0:T(8,128)(2,1)} %get-tuple-element.64.down, ...), custom_call_target="tpu_custom_call" | custom-call | tf_op jit(solution)/shard_map/pack/pallas_call | solution.py:1777

commit v2 on v1

--- a/solution.py
+++ b/solution.py
@@ -1579,9 +1579,9 @@
         qkv_g[t] = tn(left, pg_sorted[...].reshape(length, 3 * LANES)).astype(jnp.bfloat16)
         return carry
 
-    sums_done()
     lax.fori_loop(0, 4, qkv_block, 0)
     qkv_z.start()
+    sums_done()
     gu_z.step2()
     pl.semaphore_wait(free, 3)
     grads = Reduce(place, mine, theirs, first, out, second, reduce_sem)

time: 315 us -> 313 us (level)
  no operation moved by 1% of the time
where the time goes in v2:
time: 313 us; the launch traced here: 312 us
  Pallas kernels  304 us (97%)
  local copies, waits for them, and re-layouts  5.07 us (2%)
    pallas_call x1, Pallas kernels, front_moves(): pl.pallas_call(front_kernel, out_shape=(shape((rows, width), f32), shape(...  174 us
    pallas_call x1, Pallas kernels, back_moves(): pl.pallas_call(back_moves_kernel, out_shape=(shape((rows, width), f32), s...  113 us
    pallas_call x1, Pallas kernels, pack(): pl.pallas_call(pack_kernel, grid=(n,), out_shape=(shape((n * down.shape[1...  17.3 us

profile of v2, /device:TPU:0, one launch (start us, length us, event | category | flops | bytes accessed | tf_op | source)
XLA Modules:
  0.0 311.7 jit_solution(15937343692874362626)
XLA Ops:
  0.6 1.2 dynamic-slice_bitcast_fusion.6
  1.8 1.1 dynamic-slice_bitcast_fusion.4
  2.9 0.9 pad_maximum_fusion.1.qkv_own
  3.8 1.8 dynamic-slice_bitcast_fusion.3
  5.6 1.0 pad_maximum_fusion
  6.6 1.0 copy.21
  7.6 173.7 %front_moves.1 = (f32[192,1536]{1,0:T(8,128)}, f32[1,1536]{1,0:T(1,128)}, s32[8,8,128]{2,1,0:T(8,128)}, f32[2,1536]{1,0:T(2,128)}, bf16[128,1536]{1,0:T(8,128)(2...) custom-call(bf16[192,1536]{1,0:T(8,128)(2,1)} %bitcast.30, ...), custom_call_target="tpu_custom_call" | custom-call | tf_op jit(solution)/shard_map/front_moves/pallas_call | solution.py:1388
  181.3 112.9 %back_moves.1 = (f32[192,1536]{1,0:T(8,128)}, bf16[192,1536]{1,0:T(8,128)(2,1)}, f32[1,384]{1,0:T(1,128)}, f32[1,384]{1,0:T(1,128)}, bf16[8,128,1536]{2,1,0:T(8,...) custom-call(bf16[192,1536]{1,0:T(8,128)(2,1)} %bitcast.31, ...), custom_call_target="tpu_custom_call" | custom-call | tf_op jit(solution)/shard_map/back_moves/pallas_call | solution.py:1689
  294.2 17.3 %pack.1 = (f32[1024,1536]{1,0:T(8,128)}, f32[24576,128]{1,0:T(8,128)}, f32[384,1536]{1,0:T(8,128)}, f32[384,3072]{1,0:T(8,128)}, f32[192,1536]{1,0:T(8,128)}, /*...) custom-call(bf16[8,128,1536]{2,1,0:T(8,128)(2,1)} %get-tuple-element.64.down, ...), custom_call_target="tpu_custom_call" | custom-call | tf_op jit(solution)/shard_map/pack/pallas_call | solution.py:1777

commit v3 on v2

--- a/solution.py
+++ b/solution.py
@@ -1415,9 +1415,9 @@
     gu_i, middle_grad_i, hidden_i, down_i, k_i, q_i, v_i, agrad_i, att_i, lse_i, turn_i, normed_i, middle_i, qkv_i, mcols_i, low_i,
     grad, result, attn_sum, ffn_sum, down_all, gu_all, out_all, qkv_all,
     spots_s, agrad_at, gu_g, hidden, down_w, k_ref, q_ref, v_ref, agrad, att_ref, lse_ref, turn_ref, normed_in, middle, qkv_w, mcols_in, low_in, out_g, qkv_g, gu_r, out_r, qkv_r,
-    mine, theirs, first, out, second, dk_ref, dv_ref, pg_sorted, mcols,
+    mine, theirs, first, out, second, theirs2, first2, out2, second2, dk_ref, dv_ref, pg_sorted, mcols,
     gain_sum, mine_gain, ctx_gain, plane_sum, plane_gain,
-    free, local_sem, sum_sem, reduce_sem, gu_zs, out_zs, qkv_zs, down_cs, gu_cs, out_cs, qkv_cs,
+    local_sem, sum_sem, reduce_sem, gu_zs, out_zs, qkv_zs, down_cs, gu_cs, out_cs, qkv_cs,
     gain_sem, plane_sem,
 ):
     place = Place()
@@ -1483,8 +1483,6 @@
     def sums_done():
         sums.total(finish_rows)
         sums.finish()
-        for rank in (place.p, place.x, place.y):
-            pl.semaphore_signal(free, inc=1, device_id={"ctx": rank}, device_id_type=MESH)
 
     def columns_done():
         loads[13].wait()
@@ -1581,10 +1579,7 @@
 
     lax.fori_loop(0, 4, qkv_block, 0)
     qkv_z.start()
-    sums_done()
-    gu_z.step2()
-    pl.semaphore_wait(free, 3)
-    grads = Reduce(place, mine, theirs, first, out, second, reduce_sem)
+    grads = Reduce(place, mine, theirs2, first2, out2, second2, reduce_sem)
 
     def chunk(i):
         at = lax.div(spots_s[flip(place, i), 0, 0], half)
@@ -1592,7 +1587,7 @@
         return nt(rows_of, qkv_w[...].reshape(width, -1))
 
     def push(k, carry):
-        theirs[k] = chunk(2 * k + 1).astype(jnp.bfloat16)
+        theirs2[k] = chunk(2 * k + 1).astype(jnp.bfloat16)
         grads.push(k)
         return carry
 
@@ -1601,6 +1596,8 @@
         return carry
 
     lax.fori_loop(0, 4, push, 0)
+    sums_done()
+    gu_z.step2()
     lax.fori_loop(0, 4, keep, 0)
     grads.across()
     grads.beside()
@@ -1696,12 +1693,12 @@
         + [pltpu.VMEM((planes,) + part, bf) for part in parts[1:]]
         + [pltpu.VMEM((planes + 1,) + part, bf) for part in parts]
         + [
-            pltpu.VMEM((4, rows, width), f32), quads, quads, halves, halves,
+            pltpu.VMEM((4, rows, width), f32), quads, quads, halves, halves, quads, quads, halves, halves,
             pltpu.VMEM((length, LANES), f32), pltpu.VMEM((length, LANES), f32), pltpu.VMEM((16, 96, 3 * LANES), bf),
             pltpu.VMEM((n, rows, rows), bf),
             pltpu.VMEM((1, width), f32), pltpu.VMEM(small, f32), pltpu.VMEM((n,) + small, f32),
             pltpu.VMEM(small, f32), pltpu.VMEM((planes,) + small, f32),
-            pltpu.SemaphoreType.REGULAR, dma((17,)), dma((2, Reduce.sems)), dma((2, Reduce.sems)),
+            dma((17,)), dma((2, Reduce.sems)), dma((2, Reduce.sems)),
             dma((2, 5)), dma((2, 5)), dma((2, 5)), ring, ring, ring, ring, dma((2, n)), dma((2, planes)),
         ],
         compiler_params=pltpu.CompilerParams(collective_id=6, has_side_effects=True, vmem_limit_bytes=67043328),

time: 313 us -> 308 us (0.984)
  Pallas kernels: 304 us -> 300 us
    pallas_call x1, Pallas kernels: 113 us -> 109 us  [back_moves(): pl.pallas_call(back_moves_kernel, out_shape=(shape((rows, width), f32), s...]
where the time goes in v3:
time: 308 us
  Pallas kernels  300 us (97%)
  local copies, waits for them, and re-layouts  5.07 us (2%)
    pallas_call x1, Pallas kernels, front_moves(): pl.pallas_call(front_kernel, out_shape=(shape((rows, width), f32), shape(...  174 us
    pallas_call x1, Pallas kernels, back_moves(): pl.pallas_call(back_moves_kernel, out_shape=(shape((rows, width), f32), s...  109 us
    pallas_call x1, Pallas kernels, pack(): pl.pallas_call(pack_kernel, grid=(n,), out_shape=(shape((n * down.shape[1...  17.3 us

profile of v3, /device:TPU:0, one launch (start us, length us, event | category | flops | bytes accessed | tf_op | source)
XLA Modules:
  0.0 307.6 jit_solution(1667934150773809226)
XLA Ops:
  0.6 1.2 dynamic-slice_bitcast_fusion.6
  1.8 1.1 dynamic-slice_bitcast_fusion.4
  2.9 0.9 pad_maximum_fusion.1.qkv_own
  3.8 1.8 dynamic-slice_bitcast_fusion.3
  5.6 1.0 pad_maximum_fusion
  6.6 1.0 copy.21
  7.6 173.7 %front_moves.1 = (f32[192,1536]{1,0:T(8,128)}, f32[1,1536]{1,0:T(1,128)}, s32[8,8,128]{2,1,0:T(8,128)}, f32[2,1536]{1,0:T(2,128)}, bf16[128,1536]{1,0:T(8,128)(2...) custom-call(bf16[192,1536]{1,0:T(8,128)(2,1)} %bitcast.30, ...), custom_call_target="tpu_custom_call" | custom-call | tf_op jit(solution)/shard_map/front_moves/pallas_call | solution.py:1388
  181.3 108.8 %back_moves.1 = (f32[192,1536]{1,0:T(8,128)}, bf16[192,1536]{1,0:T(8,128)(2,1)}, f32[1,384]{1,0:T(1,128)}, f32[1,384]{1,0:T(1,128)}, bf16[8,128,1536]{2,1,0:T(8,...) custom-call(bf16[192,1536]{1,0:T(8,128)(2,1)} %bitcast.31, ...), custom_call_target="tpu_custom_call" | custom-call | tf_op jit(solution)/shard_map/back_moves/pallas_call | solution.py:1686
  290.1 17.3 %pack.1 = (f32[1024,1536]{1,0:T(8,128)}, f32[24576,128]{1,0:T(8,128)}, f32[384,1536]{1,0:T(8,128)}, f32[384,3072]{1,0:T(8,128)}, f32[192,1536]{1,0:T(8,128)}, /*...) custom-call(bf16[8,128,1536]{2,1,0:T(8,128)(2,1)} %get-tuple-element.64.down, ...), custom_call_target="tpu_custom_call" | custom-call | tf_op jit(solution)/shard_map/pack/pallas_call | solution.py:1774
